TPU v7x, 512 devices: a whole 4x8x8 slice. The times are simulated.
512 devices in a mesh: slab: 512 (over z, x, y, core).
Axes of the slice: x: 4, y: 8, z: 8, core: 2. Of those that a mesh axis runs over, the one named last changes fastest.
Arguments:
- start_vectors: float32 [2, 512, 256, 256], P(None, 'slab'), may hold values from -6 to 6
- levels: int32 [512, 256, 256], P('slab'), may hold values from 0 to 15
- energies: float32 [16], replicated, may hold values from -4 to 4
Outputs:
- cheb_field: float32 [2, 512, 256, 256], P(None, 'slab')
- lanczos_diag: float32 [2, 8], replicated
- lanczos_off: float32 [2, 7], replicated
- moments: float32 [2, 6], replicated
All inputs are finite; a program needn't handle non-finite values.
Results may differ from a plain program's by a relative error of at most 0.0001.
Values sent between devices are 32-bit elements; how exact they have to be, the bound alone decides.
A program may use at most 64 MiB of HBM per device.

v0:
```python
import jax
import jax.numpy as jnp
from jax import lax
from jax.sharding import Mesh
from jax.sharding import PartitionSpec as P

LANCZOS = 8
SLAB = ("slab_0", "slab_1", "slab_2", "slab_3")


def from_behind(block, axis, distance):
    devices = range(lax.axis_size(axis))
    route = [((i - distance) % len(devices), i) for i in devices]
    return lax.ppermute(block, axis, route)


def one_axis_at_a_time(value, axes):
    for axis in axes:
        value = lax.psum(value, axis)
    return value


def inner(first, second):
    return jnp.sum(first * second, axis=(1, 2, 3))


def expand(values):
    return values[:, None, None, None]


def in_plane(field):
    beside = jnp.roll(field, 1, 2) + jnp.roll(field, -1, 2)
    return beside + jnp.roll(field, 1, 3) + jnp.roll(field, -1, 3)


def hamiltonian(field, onsite):
    below_plane = from_behind(field, SLAB, 1)
    above_plane = from_behind(field, SLAB, -1)
    inside = in_plane(field)
    below = jnp.concatenate([below_plane, field[:, :-1]], axis=1)
    above = jnp.concatenate([field[:, 1:], above_plane], axis=1)
    beside = inside + below + above
    return onsite[None] * field - beside


def shards(start_vectors, levels, energies):
    level_ids = lax.broadcasted_iota(jnp.int32, (energies.shape[0], 1, 1, 1), 0)
    onsite = jnp.sum(
        jnp.where(levels[None] == level_ids, energies[:, None, None, None], 0.0), axis=0
    )
    vec_count = start_vectors.shape[0]
    norm0 = one_axis_at_a_time(inner(start_vectors, start_vectors), SLAB)
    vector = start_vectors / expand(jnp.sqrt(norm0))
    previous = jnp.zeros_like(vector)
    beta_prev = jnp.zeros((vec_count,), jnp.float32)
    alphas = []
    betas = []
    for step in range(LANCZOS):
        work = hamiltonian(vector, onsite) - expand(beta_prev) * previous
        alpha, square = (
            one_axis_at_a_time(inner(vector, work), SLAB),
            one_axis_at_a_time(inner(work, work), SLAB),
        )
        alphas.append(alpha)
        if step < LANCZOS - 1:
            work = work - expand(alpha) * vector
            beta = jnp.sqrt(square - alpha * alpha)
            betas.append(beta)
            previous, vector, beta_prev = (vector, work / expand(beta), beta)
    diag = jnp.stack(alphas, axis=1)
    offd = jnp.stack(betas, axis=1)
    zero_col = jnp.zeros((vec_count, 1), jnp.float32)
    left = jnp.concatenate([zero_col, offd], axis=1)
    right = jnp.concatenate([offd, zero_col], axis=1)
    emin = jnp.min(diag - left - right, axis=1)
    emax = jnp.max(diag + left + right, axis=1)
    center = expand((emax + emin) * 0.5)
    half = expand(0.55 * (emax - emin))

    def scaled(field):
        return (hamiltonian(field, onsite) - center * field) / half

    term1 = scaled(start_vectors)
    term2 = 2.0 * scaled(term1) - start_vectors
    term3 = 2.0 * scaled(term2) - term1
    local = jnp.stack(
        [
            inner(start_vectors, term1),
            inner(start_vectors, term2),
            inner(term2, term2),
            inner(start_vectors, term3),
            inner(term3, term2),
            inner(term3, term3),
        ],
        axis=0,
    )
    sums = one_axis_at_a_time(local, SLAB)
    moments = (
        jnp.stack(
            [
                sums[0],
                sums[1],
                sums[3],
                2.0 * sums[2] - norm0,
                2.0 * sums[4] - sums[0],
                2.0 * sums[5] - norm0,
            ],
            axis=1,
        )
        / norm0[:, None]
    )
    return (term3, diag, offd, moments)


def solution(mesh):
    split = Mesh(mesh.devices.reshape(8, 4, 8, 2), ("slab_0", "slab_1", "slab_2", "slab_3"))
    in_specs = (P(None, SLAB, None, None), P(SLAB, None, None), P())
    out_specs = (P(None, SLAB, None, None), P(), P(), P())
    return jax.shard_map(
        shards, mesh=split, in_specs=in_specs, out_specs=out_specs, check_vma=False
    )
```

profile of v0, /device:TPU:1, one launch (start us, length us, event | category | flops | bytes accessed | tf_op | source)
XLA Modules:
  0.0 615.6 jit_solution(13365147373036719849)
XLA Ops:
  1.9 20.2 %psum.476 = f32[2]{0:T(128)S(1)} all-reduce(f32[2]{0:T(128)S(1)} %multiply_reduce_fusion.20), channel_id=1, replica_groups=mesh['slab_0'=8,'slab_1'=4,'slab_2'=8,'slab_3'=2] {'slab_0'}, use_global_device_ids=true, to_apply=%region_2.3 | all-reduce | flops 2 | bytes 16 | tf_op jit(solution)/shard_map/psum | solution.py:19
  22.1 8.5 %psum.477 = f32[2]{0:T(128)S(1)} all-reduce(f32[2]{0:T(128)S(1)} %psum.476), channel_id=1, replica_groups=mesh['slab_0'=8,'slab_1'=4,'slab_2'=8,'slab_3'=2] {'slab_1'}, use_global_device_ids=true, to_apply=%region_3.4 | all-reduce | flops 2 | bytes 16 | tf_op jit(solution)/shard_map/psum | solution.py:19
  30.6 13.8 %psum.478 = f32[2]{0:T(128)S(1)} all-reduce(f32[2]{0:T(128)S(1)} %psum.477), channel_id=1, replica_groups=mesh['slab_0'=8,'slab_1'=4,'slab_2'=8,'slab_3'=2] {'slab_2'}, use_global_device_ids=true, to_apply=%region_4.5 | all-reduce | flops 2 | bytes 16 | tf_op jit(solution)/shard_map/psum | solution.py:19
  44.4 12.3 %psum.479 = f32[2]{0:T(128)S(1)} all-reduce(f32[2]{0:T(128)S(1)} %psum.478), channel_id=1, replica_groups=mesh['slab_0'=8,'slab_1'=4,'slab_2'=8,'slab_3'=2] {'slab_3'}, use_global_device_ids=true, to_apply=%region_5.6 | all-reduce | flops 2 | bytes 16 | tf_op jit(solution)/shard_map/psum | solution.py:19
  64.5 7.6 %collective-permute-start.1 = (f32[2,1,256,256]{3,2,1,0:T(8,128)S(1)}, f32[2,1,256,256]{3,2,1,0:T(8,128)}, u32[]{:S(2)}, u32[]{:S(2)}) collective-permute-start(f32[2,1,256,256]{3,2,1,0:T(8,128)S(1)} %copy-done), channel_id=1, source_target_pairs={{1,0},{2,1},{3,2},{4,3},{5,4},{6,5},{7,6},{8,7},{9,8},{10,9},{11,1... | collective-permute-start | bytes 1572872 | tf_op jit(solution)/shard_map/ppermute | solution.py:14
  75.7 11.3 %all-reduce.13 = (f32[2]{0:T(128)S(1)}, f32[2]{0:T(128)S(1)}) all-reduce(f32[2]{0:T(128)S(1)} %get-tuple-element.27, f32[2]{0:T(128)S(1)} %get-tuple-element.26), channel_id=1, replica_groups=mesh['slab_0'=8,'slab_1'=4,'slab_2'=8,'slab_3'=2] {'slab_0'}, use_global_device_ids=true, to_apply=%region_12.13 | all-reduce | flops 4 | bytes 32 | tf_op jit(solution)/shard_map/psum | solution.py:19
  93.0 17.5 %all-reduce.6 = (f32[2]{0:T(128)S(1)}, f32[2]{0:T(128)S(1)}) all-reduce(f32[2]{0:T(128)S(1)} %get-tuple-element.74, f32[2]{0:T(128)S(1)} %get-tuple-element.75), channel_id=1, replica_groups=mesh['slab_0'=8,'slab_1'=4,'slab_2'=8,'slab_3'=2] {'slab_2'}, use_global_device_ids=true, to_apply=%region_14.15 | all-reduce | flops 4 | bytes 32 | tf_op jit(solution)/shard_map/psum | solution.py:19
  110.5 10.5 %all-reduce.27 = (f32[2]{0:T(128)S(1)}, f32[2]{0:T(128)S(1)}) all-reduce(f32[2]{0:T(128)S(1)} %get-tuple-element.46, f32[2]{0:T(128)S(1)} %get-tuple-element.47), channel_id=1, replica_groups=mesh['slab_0'=8,'slab_1'=4,'slab_2'=8,'slab_3'=2] {'slab_3'}, use_global_device_ids=true, to_apply=%region_15.16 | all-reduce | flops 4 | bytes 32 | tf_op jit(solution)/shard_map/psum | solution.py:19
  137.7 12.4 %all-reduce.12 = (f32[2]{0:T(128)S(1)}, f32[2]{0:T(128)S(1)}) all-reduce(f32[2]{0:T(128)S(1)} %get-tuple-element.25, f32[2]{0:T(128)S(1)} %get-tuple-element.24), channel_id=1, replica_groups=mesh['slab_0'=8,'slab_1'=4,'slab_2'=8,'slab_3'=2] {'slab_0'}, use_global_device_ids=true, to_apply=%region_22.23 | all-reduce | flops 4 | bytes 32 | tf_op jit(solution)/shard_map/psum | solution.py:19
  157.6 18.5 %all-reduce.5 = (f32[2]{0:T(128)S(1)}, f32[2]{0:T(128)S(1)}) all-reduce(f32[2]{0:T(128)S(1)} %get-tuple-element.72, f32[2]{0:T(128)S(1)} %get-tuple-element.73), channel_id=1, replica_groups=mesh['slab_0'=8,'slab_1'=4,'slab_2'=8,'slab_3'=2] {'slab_2'}, use_global_device_ids=true, to_apply=%region_24.25 | all-reduce | flops 4 | bytes 32 | tf_op jit(solution)/shard_map/psum | solution.py:19
  196.6 11.6 %all-reduce.11 = (f32[2]{0:T(128)S(1)}, f32[2]{0:T(128)S(1)}) all-reduce(f32[2]{0:T(128)S(1)} %get-tuple-element.23, f32[2]{0:T(128)S(1)} %get-tuple-element.22), channel_id=1, replica_groups=mesh['slab_0'=8,'slab_1'=4,'slab_2'=8,'slab_3'=2] {'slab_0'}, use_global_device_ids=true, to_apply=%region_32.33 | all-reduce | flops 4 | bytes 32 | tf_op jit(solution)/shard_map/psum | solution.py:19
  215.8 19.2 %all-reduce.4 = (f32[2]{0:T(128)S(1)}, f32[2]{0:T(128)S(1)}) all-reduce(f32[2]{0:T(128)S(1)} %get-tuple-element.70, f32[2]{0:T(128)S(1)} %get-tuple-element.71), channel_id=1, replica_groups=mesh['slab_0'=8,'slab_1'=4,'slab_2'=8,'slab_3'=2] {'slab_2'}, use_global_device_ids=true, to_apply=%region_34.35 | all-reduce | flops 4 | bytes 32 | tf_op jit(solution)/shard_map/psum | solution.py:19
  254.8 12.4 %all-reduce.10 = (f32[2]{0:T(128)S(1)}, f32[2]{0:T(128)S(1)}) all-reduce(f32[2]{0:T(128)S(1)} %get-tuple-element.21, f32[2]{0:T(128)S(1)} %get-tuple-element.20), channel_id=1, replica_groups=mesh['slab_0'=8,'slab_1'=4,'slab_2'=8,'slab_3'=2] {'slab_0'}, use_global_device_ids=true, to_apply=%region_42.43 | all-reduce | flops 4 | bytes 32 | tf_op jit(solution)/shard_map/psum | solution.py:19
  274.7 18.5 %all-reduce.3 = (f32[2]{0:T(128)S(1)}, f32[2]{0:T(128)S(1)}) all-reduce(f32[2]{0:T(128)S(1)} %get-tuple-element.68, f32[2]{0:T(128)S(1)} %get-tuple-element.69), channel_id=1, replica_groups=mesh['slab_0'=8,'slab_1'=4,'slab_2'=8,'slab_3'=2] {'slab_2'}, use_global_device_ids=true, to_apply=%region_44.45 | all-reduce | flops 4 | bytes 32 | tf_op jit(solution)/shard_map/psum | solution.py:19
  313.7 11.6 %all-reduce.9 = (f32[2]{0:T(128)S(1)}, f32[2]{0:T(128)S(1)}) all-reduce(f32[2]{0:T(128)S(1)} %get-tuple-element.19, f32[2]{0:T(128)S(1)} %get-tuple-element.18), channel_id=1, replica_groups=mesh['slab_0'=8,'slab_1'=4,'slab_2'=8,'slab_3'=2] {'slab_0'}, use_global_device_ids=true, to_apply=%region_52.53 | all-reduce | flops 4 | bytes 32 | tf_op jit(solution)/shard_map/psum | solution.py:19
  332.8 19.2 %all-reduce.2 = (f32[2]{0:T(128)S(1)}, f32[2]{0:T(128)S(1)}) all-reduce(f32[2]{0:T(128)S(1)} %get-tuple-element.66, f32[2]{0:T(128)S(1)} %get-tuple-element.67), channel_id=1, replica_groups=mesh['slab_0'=8,'slab_1'=4,'slab_2'=8,'slab_3'=2] {'slab_2'}, use_global_device_ids=true, to_apply=%region_54.55 | all-reduce | flops 4 | bytes 32 | tf_op jit(solution)/shard_map/psum | solution.py:19
  371.8 12.4 %all-reduce.8 = (f32[2]{0:T(128)S(1)}, f32[2]{0:T(128)S(1)}) all-reduce(f32[2]{0:T(128)S(1)} %get-tuple-element.17, f32[2]{0:T(128)S(1)} %get-tuple-element.16), channel_id=1, replica_groups=mesh['slab_0'=8,'slab_1'=4,'slab_2'=8,'slab_3'=2] {'slab_0'}, use_global_device_ids=true, to_apply=%region_62.63 | all-reduce | flops 4 | bytes 32 | tf_op jit(solution)/shard_map/psum | solution.py:19
  391.8 18.5 %all-reduce.1 = (f32[2]{0:T(128)S(1)}, f32[2]{0:T(128)S(1)}) all-reduce(f32[2]{0:T(128)S(1)} %get-tuple-element.64, f32[2]{0:T(128)S(1)} %get-tuple-element.65), channel_id=1, replica_groups=mesh['slab_0'=8,'slab_1'=4,'slab_2'=8,'slab_3'=2] {'slab_2'}, use_global_device_ids=true, to_apply=%region_64.65 | all-reduce | flops 4 | bytes 32 | tf_op jit(solution)/shard_map/psum | solution.py:19
  431.6 11.6 %all-reduce.7 = (f32[2]{0:T(128)S(1)}, f32[2]{0:T(128)S(1)}) all-reduce(f32[2]{0:T(128)S(1)} %get-tuple-element.15, f32[2]{0:T(128)S(1)} %get-tuple-element.14), channel_id=1, replica_groups=mesh['slab_0'=8,'slab_1'=4,'slab_2'=8,'slab_3'=2] {'slab_0'}, use_global_device_ids=true, to_apply=%region_72.73 | all-reduce | flops 4 | bytes 32 | tf_op jit(solution)/shard_map/psum | solution.py:19
  450.8 19.1 %all-reduce = (f32[2]{0:T(128)S(1)}, f32[2]{0:T(128)S(1)}) all-reduce(f32[2]{0:T(128)S(1)} %get-tuple-element.62, f32[2]{0:T(128)S(1)} %get-tuple-element.63), channel_id=1, replica_groups=mesh['slab_0'=8,'slab_1'=4,'slab_2'=8,'slab_3'=2] {'slab_2'}, use_global_device_ids=true, to_apply=%region_74.75 | all-reduce | flops 4 | bytes 32 | tf_op jit(solution)/shard_map/psum | solution.py:19
  490.9 12.4 %psum.536 = f32[2]{0:T(128)S(1)} all-reduce(f32[2]{0:T(128)S(1)} %fusion.69), channel_id=1, replica_groups=mesh['slab_0'=8,'slab_1'=4,'slab_2'=8,'slab_3'=2] {'slab_0'}, use_global_device_ids=true, to_apply=%region_77.78 | all-reduce | flops 2 | bytes 16 | tf_op jit(solution)/shard_map/psum | solution.py:19
  511.0 18.5 %psum.538 = f32[2]{0:T(128)S(1)} all-reduce(f32[2]{0:T(128)S(1)} %psum.537), channel_id=1, replica_groups=mesh['slab_0'=8,'slab_1'=4,'slab_2'=8,'slab_3'=2] {'slab_2'}, use_global_device_ids=true, to_apply=%region_79.80 | all-reduce | flops 2 | bytes 16 | tf_op jit(solution)/shard_map/psum | solution.py:19
  565.2 11.9 %psum.540 = f32[6,2]{0,1:T(2,128)S(1)} all-reduce(f32[6,2]{0,1:T(2,128)S(1)} %stack.105), channel_id=1, replica_groups=mesh['slab_0'=8,'slab_1'=4,'slab_2'=8,'slab_3'=2] {'slab_0'}, use_global_device_ids=true, to_apply=%region_89.90 | all-reduce | flops 12 | bytes 96 | tf_op jit(solution)/shard_map/psum | solution.py:19
  584.5 24.9 %psum.542 = f32[6,2]{0,1:T(2,128)S(1)} all-reduce(f32[6,2]{0,1:T(2,128)S(1)} %psum.541), channel_id=1, replica_groups=mesh['slab_0'=8,'slab_1'=4,'slab_2'=8,'slab_3'=2] {'slab_2'}, use_global_device_ids=true, to_apply=%region_91.92 | all-reduce | flops 12 | bytes 96 | tf_op jit(solution)/shard_map/psum | solution.py:19
  (216 shorter events, 259.8 us)
Async XLA Ops:
  0.6 56.1 %copy-start = (f32[2,1,256,256]{3,2,1,0:T(8,128)S(1)}, f32[2,1,256,256]{3,2,1,0:T(8,128)}, u32[]{:S(2)}) copy-start(f32[2,1,256,256]{3,2,1,0:T(8,128)} %param.3) | copy-start | bytes 1572868
  56.9 18.3 %collective-permute-start.2 = (f32[2,1,256,256]{3,2,1,0:T(8,128)S(1)}, f32[2,1,256,256]{3,2,1,0:T(8,128)S(1)}, u32[]{:S(2)}, u32[]{:S(2)}) collective-permute-start(f32[2,1,256,256]{3,2,1,0:T(8,128)S(1)} %broadcast_divide_fusion), channel_id=1, source_target_pairs={{511,0},{0,1},{1,2},{2,3},{3,4},{4,5},{5,6},{6,7},{7,8},{8,9},{9,1... | collective-permute-start | bytes 1572872 | tf_op jit(solution)/shard_map/ppermute | solution.py:14
  58.9 16.3 %collective-permute-start.3 = (f32[2,1,256,256]{3,2,1,0:T(8,128)S(1)}, f32[2,1,256,256]{3,2,1,0:T(8,128)S(1)}, u32[]{:S(2)}, u32[]{:S(2)}) collective-permute-start(f32[2,1,256,256]{3,2,1,0:T(8,128)S(1)} %broadcast_divide_fusion), channel_id=1, source_target_pairs={{1,0},{2,1},{3,2},{4,3},{5,4},{6,5},{7,6},{8,7},{9,8},{10,9},{11,1... | collective-permute-start | bytes 1572872 | tf_op jit(solution)/shard_map/ppermute | solution.py:14
  61.2 472.5 %collective-permute-start = (f32[2,1,256,256]{3,2,1,0:T(8,128)S(1)}, f32[2,1,256,256]{3,2,1,0:T(8,128)}, u32[]{:S(2)}, u32[]{:S(2)}) collective-permute-start(f32[2,1,256,256]{3,2,1,0:T(8,128)S(1)} %copy-done), channel_id=1, source_target_pairs={{511,0},{0,1},{1,2},{2,3},{3,4},{4,5},{5,6},{6,7},{7,8},{8,9},{9,1... | collective-permute-start | bytes 1572872 | tf_op jit(solution)/shard_map/ppermute | solution.py:14
  64.5 469.3 %collective-permute-start.1 = (f32[2,1,256,256]{3,2,1,0:T(8,128)S(1)}, f32[2,1,256,256]{3,2,1,0:T(8,128)}, u32[]{:S(2)}, u32[]{:S(2)}) collective-permute-start(f32[2,1,256,256]{3,2,1,0:T(8,128)S(1)} %copy-done), channel_id=1, source_target_pairs={{1,0},{2,1},{3,2},{4,3},{5,4},{6,5},{7,6},{8,7},{9,8},{10,9},{11,1... | collective-permute-start | bytes 1572872 | tf_op jit(solution)/shard_map/ppermute | solution.py:14
  121.2 10.0 %collective-permute-start.4 = (f32[2,1,256,256]{3,2,1,0:T(8,128)S(1)}, f32[2,1,256,256]{3,2,1,0:T(8,128)S(1)}, u32[]{:S(2)}, u32[]{:S(2)}) collective-permute-start(f32[2,1,256,256]{3,2,1,0:T(8,128)S(1)} %subtract_divide_fusion.6), channel_id=1, source_target_pairs={{511,0},{0,1},{1,2},{2,3},{3,4},{4,5},{5,6},{6,7},{7,8},{8,9},{9,1... | collective-permute-start | bytes 1572872 | tf_op jit(solution)/shard_map/ppermute | solution.py:14
  125.1 10.8 %collective-permute-start.5 = (f32[2,1,256,256]{3,2,1,0:T(8,128)S(1)}, f32[2,1,256,256]{3,2,1,0:T(8,128)}, u32[]{:S(2)}, u32[]{:S(2)}) collective-permute-start(f32[2,1,256,256]{3,2,1,0:T(8,128)S(1)} %subtract_divide_fusion.6), channel_id=1, source_target_pairs={{1,0},{2,1},{3,2},{4,3},{5,4},{6,5},{7,6},{8,7},{9,8},{10,9},{11,1... | collective-permute-start | bytes 1572872 | tf_op jit(solution)/shard_map/ppermute | solution.py:14
  180.1 10.0 %collective-permute-start.6 = (f32[2,1,256,256]{3,2,1,0:T(8,128)S(1)}, f32[2,1,256,256]{3,2,1,0:T(8,128)S(1)}, u32[]{:S(2)}, u32[]{:S(2)}) collective-permute-start(f32[2,1,256,256]{3,2,1,0:T(8,128)S(1)} %subtract_divide_fusion.5), channel_id=1, source_target_pairs={{511,0},{0,1},{1,2},{2,3},{3,4},{4,5},{5,6},{6,7},{7,8},{8,9},{9,1... | collective-permute-start | bytes 1572872 | tf_op jit(solution)/shard_map/ppermute | solution.py:14
  184.0 10.8 %collective-permute-start.7 = (f32[2,1,256,256]{3,2,1,0:T(8,128)S(1)}, f32[2,1,256,256]{3,2,1,0:T(8,128)}, u32[]{:S(2)}, u32[]{:S(2)}) collective-permute-start(f32[2,1,256,256]{3,2,1,0:T(8,128)S(1)} %subtract_divide_fusion.5), channel_id=1, source_target_pairs={{1,0},{2,1},{3,2},{4,3},{5,4},{6,5},{7,6},{8,7},{9,8},{10,9},{11,1... | collective-permute-start | bytes 1572872 | tf_op jit(solution)/shard_map/ppermute | solution.py:14
  238.3 10.0 %collective-permute-start.8 = (f32[2,1,256,256]{3,2,1,0:T(8,128)S(1)}, f32[2,1,256,256]{3,2,1,0:T(8,128)S(1)}, u32[]{:S(2)}, u32[]{:S(2)}) collective-permute-start(f32[2,1,256,256]{3,2,1,0:T(8,128)S(1)} %subtract_divide_fusion.4), channel_id=1, source_target_pairs={{511,0},{0,1},{1,2},{2,3},{3,4},{4,5},{5,6},{6,7},{7,8},{8,9},{9,1... | collective-permute-start | bytes 1572872 | tf_op jit(solution)/shard_map/ppermute | solution.py:14
  242.2 10.8 %collective-permute-start.9 = (f32[2,1,256,256]{3,2,1,0:T(8,128)S(1)}, f32[2,1,256,256]{3,2,1,0:T(8,128)}, u32[]{:S(2)}, u32[]{:S(2)}) collective-permute-start(f32[2,1,256,256]{3,2,1,0:T(8,128)S(1)} %subtract_divide_fusion.4), channel_id=1, source_target_pairs={{1,0},{2,1},{3,2},{4,3},{5,4},{6,5},{7,6},{8,7},{9,8},{10,9},{11,1... | collective-permute-start | bytes 1572872 | tf_op jit(solution)/shard_map/ppermute | solution.py:14
  297.2 10.0 %collective-permute-start.10 = (f32[2,1,256,256]{3,2,1,0:T(8,128)S(1)}, f32[2,1,256,256]{3,2,1,0:T(8,128)S(1)}, u32[]{:S(2)}, u32[]{:S(2)}) collective-permute-start(f32[2,1,256,256]{3,2,1,0:T(8,128)S(1)} %subtract_divide_fusion.3), channel_id=1, source_target_pairs={{511,0},{0,1},{1,2},{2,3},{3,4},{4,5},{5,6},{6,7},{7,8},{8,9},{9,1... | collective-permute-start | bytes 1572872 | tf_op jit(solution)/shard_map/ppermute | solution.py:14
  301.1 10.8 %collective-permute-start.11 = (f32[2,1,256,256]{3,2,1,0:T(8,128)S(1)}, f32[2,1,256,256]{3,2,1,0:T(8,128)}, u32[]{:S(2)}, u32[]{:S(2)}) collective-permute-start(f32[2,1,256,256]{3,2,1,0:T(8,128)S(1)} %subtract_divide_fusion.3), channel_id=1, source_target_pairs={{1,0},{2,1},{3,2},{4,3},{5,4},{6,5},{7,6},{8,7},{9,8},{10,9},{11,1... | collective-permute-start | bytes 1572872 | tf_op jit(solution)/shard_map/ppermute | solution.py:14
  355.3 10.0 %collective-permute-start.12 = (f32[2,1,256,256]{3,2,1,0:T(8,128)S(1)}, f32[2,1,256,256]{3,2,1,0:T(8,128)S(1)}, u32[]{:S(2)}, u32[]{:S(2)}) collective-permute-start(f32[2,1,256,256]{3,2,1,0:T(8,128)S(1)} %subtract_divide_fusion.2), channel_id=1, source_target_pairs={{511,0},{0,1},{1,2},{2,3},{3,4},{4,5},{5,6},{6,7},{7,8},{8,9},{9,1... | collective-permute-start | bytes 1572872 | tf_op jit(solution)/shard_map/ppermute | solution.py:14
  359.2 10.8 %collective-permute-start.13 = (f32[2,1,256,256]{3,2,1,0:T(8,128)S(1)}, f32[2,1,256,256]{3,2,1,0:T(8,128)}, u32[]{:S(2)}, u32[]{:S(2)}) collective-permute-start(f32[2,1,256,256]{3,2,1,0:T(8,128)S(1)} %subtract_divide_fusion.2), channel_id=1, source_target_pairs={{1,0},{2,1},{3,2},{4,3},{5,4},{6,5},{7,6},{8,7},{9,8},{10,9},{11,1... | collective-permute-start | bytes 1572872 | tf_op jit(solution)/shard_map/ppermute | solution.py:14
  414.3 10.0 %collective-permute-start.14 = (f32[2,1,256,256]{3,2,1,0:T(8,128)S(1)}, f32[2,1,256,256]{3,2,1,0:T(8,128)}, u32[]{:S(2)}, u32[]{:S(2)}) collective-permute-start(f32[2,1,256,256]{3,2,1,0:T(8,128)S(1)} %subtract_divide_fusion.1), channel_id=1, source_target_pairs={{511,0},{0,1},{1,2},{2,3},{3,4},{4,5},{5,6},{6,7},{7,8},{8,9},{9,1... | collective-permute-start | bytes 1572872 | tf_op jit(solution)/shard_map/ppermute | solution.py:14
  418.1 10.9 %collective-permute-start.15 = (f32[2,1,256,256]{3,2,1,0:T(8,128)S(1)}, f32[2,1,256,256]{3,2,1,0:T(8,128)}, u32[]{:S(2)}, u32[]{:S(2)}) collective-permute-start(f32[2,1,256,256]{3,2,1,0:T(8,128)S(1)} %subtract_divide_fusion.1), channel_id=1, source_target_pairs={{1,0},{2,1},{3,2},{4,3},{5,4},{6,5},{7,6},{8,7},{9,8},{10,9},{11,1... | collective-permute-start | bytes 1572872 | tf_op jit(solution)/shard_map/ppermute | solution.py:14
  474.3 10.0 %collective-permute-start.16 = (f32[2,1,256,256]{3,2,1,0:T(8,128)S(1)}, f32[2,1,256,256]{3,2,1,0:T(8,128)S(1)}, u32[]{:S(2)}, u32[]{:S(2)}) collective-permute-start(f32[2,1,256,256]{3,2,1,0:T(8,128)S(1)} %subtract_divide_fusion), channel_id=1, source_target_pairs={{511,0},{0,1},{1,2},{2,3},{3,4},{4,5},{5,6},{6,7},{7,8},{8,9},{9,1... | collective-permute-start | bytes 1572872 | tf_op jit(solution)/shard_map/ppermute | solution.py:14
  478.2 10.8 %collective-permute-start.17 = (f32[2,1,256,256]{3,2,1,0:T(8,128)S(1)}, f32[2,1,256,256]{3,2,1,0:T(8,128)}, u32[]{:S(2)}, u32[]{:S(2)}) collective-permute-start(f32[2,1,256,256]{3,2,1,0:T(8,128)S(1)} %subtract_divide_fusion), channel_id=1, source_target_pairs={{1,0},{2,1},{3,2},{4,3},{5,4},{6,5},{7,6},{8,7},{9,8},{10,9},{11,1... | collective-permute-start | bytes 1572872 | tf_op jit(solution)/shard_map/ppermute | solution.py:14
  489.0 44.7 %copy-start.1 = (f32[2,1,255,256]{3,2,1,0:T(8,128)S(1)}, f32[2,1,255,256]{3,2,1,0:T(8,128)}, u32[]{:S(2)}) copy-start(f32[2,1,255,256]{3,2,1,0:T(8,128)} %get-tuple-element.182) | copy-start | bytes 1566724
  535.6 10.0 %collective-permute-start.18 = (f32[2,1,256,256]{3,2,1,0:T(8,128)S(1)}, f32[2,1,256,256]{3,2,1,0:T(8,128)S(1)}, u32[]{:S(2)}, u32[]{:S(2)}) collective-permute-start(f32[2,1,256,256]{3,2,1,0:T(8,128)S(1)} %fusion.6), channel_id=1, source_target_pairs={{511,0},{0,1},{1,2},{2,3},{3,4},{4,5},{5,6},{6,7},{7,8},{8,9},{9,1... | collective-permute-start | bytes 1572872 | tf_op jit(solution)/shard_map/ppermute | solution.py:14
  539.5 10.8 %collective-permute-start.19 = (f32[2,1,256,256]{3,2,1,0:T(8,128)S(1)}, f32[2,1,256,256]{3,2,1,0:T(8,128)S(1)}, u32[]{:S(2)}, u32[]{:S(2)}) collective-permute-start(f32[2,1,256,256]{3,2,1,0:T(8,128)S(1)} %fusion.6), channel_id=1, source_target_pairs={{1,0},{2,1},{3,2},{4,3},{5,4},{6,5},{7,6},{8,7},{9,8},{10,9},{11,1... | collective-permute-start | bytes 1572872 | tf_op jit(solution)/shard_map/ppermute | solution.py:14
  550.8 8.0 %collective-permute-start.20 = (f32[2,1,256,256]{3,2,1,0:T(8,128)S(1)}, f32[2,1,256,256]{3,2,1,0:T(8,128)S(1)}, u32[]{:S(2)}, u32[]{:S(2)}) collective-permute-start(f32[2,1,256,256]{3,2,1,0:T(8,128)S(1)} %multiply_subtract_fusion.1), channel_id=1, source_target_pairs={{511,0},{0,1},{1,2},{2,3},{3,4},{4,5},{5,6},{6,7},{7,8},{8,9},{9,1... | collective-permute-start | bytes 1572872 | tf_op jit(solution)/shard_map/ppermute | solution.py:14
  552.7 10.5 %collective-permute-start.21 = (f32[2,1,256,256]{3,2,1,0:T(8,128)S(1)}, f32[2,1,256,256]{3,2,1,0:T(8,128)S(1)}, u32[]{:S(2)}, u32[]{:S(2)}) collective-permute-start(f32[2,1,256,256]{3,2,1,0:T(8,128)S(1)} %multiply_subtract_fusion.1), channel_id=1, source_target_pairs={{1,0},{2,1},{3,2},{4,3},{5,4},{6,5},{7,6},{8,7},{9,8},{10,9},{11,1... | collective-permute-start | bytes 1572872 | tf_op jit(solution)/shard_map/ppermute | solution.py:14
  (21 other events, 124.8 us)
where the time goes:
time: 617 us; the launch traced here: 616 us
  blocking collectives  442 us (72%)
  starting transfers between devices  68.7 us (11%)
  waiting for transfers between devices  66.6 us (11%)
  other arithmetic  22.6 us (4%)
  local copies, waits for them, and re-layouts  14.3 us (2%)
    psum x40, blocking collectives, one_axis_at_a_time(): value = lax.psum(value, axis)  442 us
    ppermute x22, starting transfers between devices, from_behind(): return lax.ppermute(block, axis, route)  68.7 us
    ppermute x22, waiting for transfers between devices, from_behind(): return lax.ppermute(block, axis, route)  66.6 us
    reduce_sum x10, other arithmetic, inner(): return jnp.sum(first * second, axis=(1, 2, 3))  16.6 us
  transfers between devices with their start and end apart: 22, of which 18 were waited for; matrix products, arithmetic and copies ran while one was open for 5% of the time, Pallas kernels for 0%

commit v1 on v0

v1 whole, which is shorter than its diff:
```python
import functools

import jax
import jax.numpy as jnp
from jax import lax
from jax.experimental import pallas as pl
from jax.experimental.pallas import tpu as pltpu
from jax.sharding import PartitionSpec as P

STEPS = 8
CHUNKS = 2
BLOCK = 32
MESH = pl.DeviceIdType.MESH


def two_sum(a, b):
    s = a + b
    t = s - a
    return s, (a - (s - t)) + (b - t)


def fast_two_sum(a, b):
    s = a + b
    return s, b - (s - a)


def split(a):
    t = a * 4097.0
    high = t - (t - a)
    return high, a - high


def two_prod(a, b):
    p = a * b
    ah, al = split(a)
    bh, bl = split(b)
    return p, ((ah * bh - p) + ah * bl + al * bh) + al * bl


def pair_add(a, b):
    s, e = two_sum(a[0], b[0])
    return fast_two_sum(s, e + (a[1] + b[1]))


def pair_neg(a):
    return -a[0], -a[1]


def pair_sub(a, b):
    return pair_add(a, pair_neg(b))


def pair_mul(a, b):
    p, e = two_prod(a[0], b[0])
    return fast_two_sum(p, e + (a[0] * b[1] + a[1] * b[0]))


def pair_div(a, b):
    inv = 1.0 / b[0]
    first = a[0] * inv
    p, e = two_prod(first, b[0])
    rest = (a[0] - p) - e + a[1] - first * b[1]
    return fast_two_sum(first, rest * inv)


def tree_rows(rows):
    lost = None
    while len(rows) > 1:
        sums = []
        for a, b in zip(rows[::2], rows[1::2]):
            s, e = two_sum(a, b)
            sums.append(s)
            lost = e if lost is None else lost + e
        rows = sums
    return rows[0], lost


def coefficients(norms, crosses):
    nu = []
    for k in range(STEPS):
        if k == 0:
            nu += [norms[0], crosses[0]]
        elif k < STEPS - 1:
            nu += [pair_sub(norms[k], norms[k - 1]), pair_sub(crosses[k], crosses[k - 1])]
        else:
            twice = pair_add(crosses[k - 1], crosses[k - 1])
            nu += [pair_sub(norms[k], norms[k - 1]), pair_sub(crosses[k], twice)]
    older, old = {}, dict(enumerate(nu))
    ratio = pair_div(old[1], old[0])
    diag, square = [ratio], []
    for k in range(1, STEPS):
        new = {}
        for l in range(k, 2 * STEPS - k):
            term = pair_sub(pair_add(old[l + 1], old[l - 1]), pair_mul(diag[-1], old[l]))
            if k > 1:
                term = pair_sub(term, pair_mul(square[-1], older[l]))
            new[l] = term
        square.append(pair_div(new[k], old[k - 1]))
        next_ratio = pair_div(new[k + 1], new[k])
        diag.append(pair_sub(next_ratio, ratio))
        ratio = next_ratio
        older, old = old, new
    return diag, square


def kernel(
    n,
    group,
    sv_ref,
    lev_ref,
    en_ref,
    field_ref,
    diag_ref,
    off_ref,
    mom_ref,
    basis,
    below,
    above,
    onsite,
    levels,
    gathered,
    row_a,
    row_b,
    near,
    far,
    table,
    load_sem,
    up_send,
    up_recv,
    down_send,
    down_recv,
    near_send,
    near_recv,
    far_send,
    far_recv,
):
    ny, nx = onsite.shape
    rows = ny // CHUNKS
    groups = n // group
    me = lax.axis_index("slab")
    up = lax.rem(me + 1, n)
    down = lax.rem(me + n - 1, n)
    mine = lax.rem(me, group)
    team = me // group

    def near_peer(k):
        place = lax.rem(mine + k, group)
        return place, team * group + place

    def far_peer(k):
        place = lax.rem(team + k, groups)
        return place, place * group + mine

    def load(v, c):
        part = pl.ds(c * rows, rows)
        return pltpu.make_async_copy(
            sv_ref.at[v, 0, part], basis.at[1, v, part], load_sem.at[v * CHUNKS + c]
        )

    load_levels = pltpu.make_async_copy(lev_ref.at[0], levels, load_sem.at[2 * CHUNKS])
    for v in range(2):
        for c in range(CHUNKS):
            load(v, c).start()
    load_levels.start()

    barrier = pltpu.get_barrier_semaphore()

    def greet(device):
        pl.semaphore_signal(barrier, inc=1, device_id=(device,), device_id_type=MESH)

    greet(up)
    greet(down)
    lax.fori_loop(1, group, lambda k, _: greet(near_peer(k)[1]), None)
    lax.fori_loop(1, groups, lambda k, _: greet(far_peer(k)[1]), None)
    pl.semaphore_wait(barrier, group + groups)

    def halo(k, v, c, upward):
        part = pl.ds(c * rows, rows)
        landing, send, recv, device = (
            (below, up_send, up_recv, up) if upward else (above, down_send, down_recv, down)
        )
        return pltpu.make_async_remote_copy(
            src_ref=basis.at[k + 1, v, part],
            dst_ref=landing.at[k, v, part],
            send_sem=send.at[k, v, c],
            recv_sem=recv.at[k, v, c],
            device_id=(device,),
            device_id_type=MESH,
        )

    for v in range(2):
        for c in range(CHUNKS):
            load(v, c).wait()
            halo(0, v, c, True).start()
            halo(0, v, c, False).start()

    energies = [en_ref[i] for i in range(en_ref.shape[0])]
    shift = sum(energies[1:], energies[0]) * (1.0 / len(energies))
    spread = sum((e - shift) * (e - shift) for e in energies) * (1.0 / len(energies))
    width_row = jnp.full((1, nx), spread + 6.0, jnp.float32)
    inv_row = 1.0 / jnp.sqrt(width_row)

    load_levels.wait()

    def place_onsite(b, _):
        part = pl.ds(pl.multiple_of(b * BLOCK, BLOCK), BLOCK)
        ids = levels[part, :]
        value = jnp.full((BLOCK, nx), energies[0], jnp.float32)
        for i in range(1, len(energies)):
            value = jnp.where(ids == i, energies[i], value)
        onsite[part, :] = (value - shift) * inv_row
        for v in range(2):
            basis[0, v, part, :] = jnp.zeros((BLOCK, nx), jnp.float32)
        return None

    lax.fori_loop(0, ny // BLOCK, place_onsite, None)
    gathered[...] = jnp.zeros((8, 128), jnp.float32)

    def fold(x):
        x = (x[0:8] + x[8:16]) + (x[16:24] + x[24:32])
        return x

    def sweep(k, v, c, totals, last):
        def block(b, carry):
            nh, nl, ch, cl = carry
            start = pl.multiple_of(c * rows + b * BLOCK, BLOCK)
            part = pl.ds(start, BLOCK)
            before = pl.ds(pl.multiple_of(lax.rem(start + (ny - 8), ny), 8), 8)
            after = pl.ds(pl.multiple_of(lax.rem(start + BLOCK, ny), 8), 8)
            here = basis[k + 1, v, part, :]
            tall = jnp.concatenate(
                [basis[k + 1, v, before, :], here, basis[k + 1, v, after, :]], axis=0
            )
            height = BLOCK + 16
            beside = pltpu.roll(tall, 1, 0)[8 : 8 + BLOCK]
            beside = beside + pltpu.roll(tall, height - 1, 0)[8 : 8 + BLOCK]
            beside = beside + (pltpu.roll(here, 1, 1) + pltpu.roll(here, nx - 1, 1))
            if last:
                one = (below if c < CHUNKS // 2 else above)[k, v, part, :]
                beside = beside + (one + one)
            else:
                beside = beside + (below[k, v, part, :] + above[k, v, part, :])
            new = onsite[part, :] * here - inv_row * beside
            if not last:
                new = new - basis[k, v, part, :]
                basis[k + 2, v, part, :] = new
            nh, e = two_sum(nh, fold(here * here))
            ch, d = two_sum(ch, fold(new * here))
            return nh, nl + e, ch, cl + d

        return lax.fori_loop(0, rows // BLOCK, block, totals)

    sub = lax.broadcasted_iota(jnp.int32, (8, 128), 0)
    lane = lax.broadcasted_iota(jnp.int32, (8, 128), 1)

    def gather(k, totals):
        high = jnp.zeros((8, 128), jnp.float32)
        low = jnp.zeros((8, 128), jnp.float32)
        for q, (h, l) in enumerate(totals):
            h, e = two_sum(h[:, :128], h[:, 128:])
            l = (l[:, :128] + l[:, 128:]) + e
            for shift_by in (4, 2, 1):
                h, e = two_sum(h, pltpu.roll(h, shift_by, 0))
                l = l + pltpu.roll(l, shift_by, 0) + e
            high = jnp.where(sub == q, h, high)
            low = jnp.where(sub == q, l, low)
        for shift_by in (64, 32, 16, 8, 4, 2, 1):
            high, e = two_sum(high, pltpu.roll(high, shift_by, 1))
            low = low + pltpu.roll(low, shift_by, 1) + e
        target = jnp.where(sub < 4, (sub // 2) * 64 + lax.rem(sub, 2) * 8 + k, 1000)
        gathered[...] += jnp.where(lane == target, high, 0.0) + jnp.where(
            lane == target + 16, low, 0.0
        )

    def step(k, final_sends=False, last=False):
        totals = []
        for v in range(2):
            zero = jnp.zeros((8, nx), jnp.float32)
            total = (zero, zero, zero, zero)
            for c in range(CHUNKS):
                if not last or c < CHUNKS // 2:
                    halo(k, v, c, True).wait_recv()
                if not last or c >= CHUNKS // 2:
                    halo(k, v, c, False).wait_recv()
                total = sweep(k, v, c, total, last)
                if not last:
                    if not final_sends or c < CHUNKS // 2:
                        halo(k + 1, v, c, True).start()
                    if not final_sends or c >= CHUNKS // 2:
                        halo(k + 1, v, c, False).start()
            totals += [total[:2], total[2:]]
        gather(k, totals)

    lax.fori_loop(0, STEPS - 2, lambda k, _: step(k), None)
    step(STEPS - 2, final_sends=True)
    step(STEPS - 1, last=True)

    packed = gathered[...]
    for shift_by in (4, 2, 1):
        packed = packed + pltpu.roll(packed, shift_by, 0)

    row_lane = lax.broadcasted_iota(jnp.int32, (1, 128), 1)
    is_high = lax.rem(row_lane, 64) < 16

    def exchange(row, staging, slots, place, peer, count, send, recv):
        def copy(k, arriving):
            other, device = peer(k)
            slot = other if arriving else place
            return pltpu.make_async_remote_copy(
                src_ref=staging,
                dst_ref=slots.at[slot],
                send_sem=send.at[k],
                recv_sem=recv.at[slot],
                device_id=(device,),
                device_id_type=MESH,
            )

        staging[...] = row
        slots[place] = row
        lax.fori_loop(1, count, lambda k, _: copy(k, False).start(), None)
        lax.fori_loop(1, count, lambda k, _: copy(k, True).wait_recv(), None)
        total, lost = tree_rows([slots[i] for i in range(count)])
        lax.fori_loop(1, count, lambda k, _: copy(k, False).wait_send(), None)
        return jnp.where(is_high, total, total + pltpu.roll(lost, 16, 1))

    row = exchange(packed[0:1], row_a, near, mine, near_peer, group, near_send, near_recv)
    row = exchange(row, row_b, far, team, far_peer, groups, far_send, far_recv)

    tall_row = lax.broadcasted_iota(jnp.int32, (32, 128), 0)
    tall_lane = lax.broadcasted_iota(jnp.int32, (32, 128), 1)
    spread_row = jnp.broadcast_to(row, (32, 128))
    first = jnp.sum(jnp.where(tall_lane == tall_row, spread_row, 0.0), axis=1, keepdims=True)
    second = jnp.sum(
        jnp.where(tall_lane == tall_row + 64, spread_row, 0.0), axis=1, keepdims=True
    )
    table[...] = jnp.where(tall_lane < 64, first, second)

    norms = [(table[k : k + 1, :], table[16 + k : 17 + k, :]) for k in range(STEPS)]
    crosses = [(table[8 + k : 9 + k, :], table[24 + k : 25 + k, :]) for k in range(STEPS)]
    diag, square = coefficients(norms, crosses)

    width = 1.0 / inv_row[:, :128]
    alphas = [shift + width * a[0] for a in diag]
    betas = [width * jnp.sqrt(b[0]) for b in square]
    zero = jnp.zeros((1, 128), jnp.float32)
    left = [zero] + betas
    right = betas + [zero]
    emin = functools.reduce(jnp.minimum, [a - p - q for a, p, q in zip(alphas, left, right)])
    emax = functools.reduce(jnp.maximum, [a + p + q for a, p, q in zip(alphas, left, right)])
    center = (emax + emin) * 0.5
    inv_half = 1.0 / (0.55 * (emax - emin))
    slope = width * inv_half
    offset = (shift - center) * inv_half

    def apply(poly):
        around = [zero] + poly + [zero]
        out = []
        for k in range(len(poly) + 1):
            value = slope * around[k] if k else None
            if k < len(poly):
                value = offset * poly[k] if value is None else value + offset * poly[k]
            if k + 2 < len(around) - 1:
                value = value + slope * around[k + 2]
            out.append(value)
        return out

    t0 = [zero + 1.0]
    t1 = apply(t0)
    t2 = [2.0 * q for q in apply(t1)]
    t2[0] = t2[0] - 1.0
    t3 = [2.0 * q for q in apply(t2)]
    t3 = [q - t1[k] if k < 2 else q for k, q in enumerate(t3)]

    inv_norm = 1.0 / norms[0][0]
    size = [q[0] * inv_norm for q in norms[:4]]
    cross = [q[0] * inv_norm for q in crosses[:3]]
    skip = pair_sub(norms[1], norms[0])[0] * inv_norm
    skip_next = pair_sub(norms[2], norms[0])[0] * inv_norm
    skip_two = pair_sub(crosses[1], crosses[0])[0] * inv_norm
    gram = [
        [zero + 1.0, cross[0], skip, skip_two],
        [cross[0], size[1], cross[1], skip_next],
        [skip, cross[1], size[2], cross[2]],
        [skip_two, skip_next, cross[2], size[3]],
    ]

    def inner(p, q):
        return sum(
            a * sum(b * gram[i][j] for j, b in enumerate(q)) for i, a in enumerate(p)
        )

    d01 = inner(t0, t1)
    moments = [
        d01,
        inner(t0, t2),
        inner(t0, t3),
        2.0 * inner(t2, t2) - 1.0,
        2.0 * inner(t3, t2) - d01,
        2.0 * inner(t3, t3) - 1.0,
    ]

    def emit(ref, values):
        packed = zero
        for k, value in enumerate(values):
            packed = jnp.where(lax.rem(row_lane, 64) == k, value, packed)
        ref[0:1, :] = packed[:, : len(values)]
        ref[1:2, :] = pltpu.roll(packed, 64, 1)[:, : len(values)]

    for v in range(2):
        keep = row_lane < 64 if v == 0 else row_lane >= 64
        scale = [jnp.where(keep, q, pltpu.roll(q, 64, 1)) for q in t3]
        scale = [jnp.concatenate([q, q], axis=1) for q in scale]

        def finish(b, _):
            part = pl.ds(pl.multiple_of(b * BLOCK, BLOCK), BLOCK)
            value = scale[0] * basis[1, v, part, :] + scale[1] * basis[2, v, part, :]
            value = value + scale[2] * basis[3, v, part, :]
            field_ref[v, 0, part, :] = value + scale[3] * basis[4, v, part, :]
            return None

        lax.fori_loop(0, ny // BLOCK, finish, None)

    emit(diag_ref, alphas)
    emit(off_ref, betas)
    emit(mom_ref, moments)

    def drain(k, _):
        for v in range(2):
            for c in range(CHUNKS):
                halo(k, v, c, True).wait_send()
                halo(k, v, c, False).wait_send()
        return None

    lax.fori_loop(0, STEPS - 1, drain, None)
    for v in range(2):
        for c in range(CHUNKS):
            halo(STEPS - 1, v, c, c < CHUNKS // 2).wait_send()


def solution(mesh):
    n = mesh.shape["slab"]
    group = 16 if n >= 128 else 4

    def shards(start_vectors, levels, energies):
        vecs, _, ny, nx = start_vectors.shape
        f32 = jnp.float32
        dma = pltpu.SemaphoreType.DMA
        vmem = pl.BlockSpec(memory_space=pltpu.VMEM)
        hbm = pl.BlockSpec(memory_space=pl.ANY)
        halo_sem = dma((STEPS, vecs, CHUNKS))
        return pl.pallas_call(
            functools.partial(kernel, n, group),
            out_shape=(
                jax.ShapeDtypeStruct(start_vectors.shape, f32),
                jax.ShapeDtypeStruct((vecs, STEPS), f32),
                jax.ShapeDtypeStruct((vecs, STEPS - 1), f32),
                jax.ShapeDtypeStruct((vecs, 6), f32),
            ),
            in_specs=[hbm, hbm, pl.BlockSpec(memory_space=pltpu.SMEM)],
            out_specs=(vmem, vmem, vmem, vmem),
            scratch_shapes=[
                pltpu.VMEM((STEPS + 1, vecs, ny, nx), f32),
                pltpu.VMEM((STEPS, vecs, ny, nx), f32),
                pltpu.VMEM((STEPS, vecs, ny, nx), f32),
                pltpu.VMEM((ny, nx), f32),
                pltpu.VMEM((ny, nx), jnp.int32),
                pltpu.VMEM((8, 128), f32),
                pltpu.VMEM((1, 128), f32),
                pltpu.VMEM((1, 128), f32),
                pltpu.VMEM((group, 1, 128), f32),
                pltpu.VMEM((n // group, 1, 128), f32),
                pltpu.VMEM((32, 128), f32),
                dma((2 * CHUNKS + 1,)),
                halo_sem,
                halo_sem,
                halo_sem,
                halo_sem,
                dma((group,)),
                dma((group,)),
                dma((n // group,)),
                dma((n // group,)),
            ],
            compiler_params=pltpu.CompilerParams(collective_id=0, has_side_effects=True),
        )(start_vectors, levels, energies)

    return jax.shard_map(
        shards,
        mesh=mesh,
        in_specs=(P(None, "slab", None, None), P("slab", None, None), P()),
        out_specs=(P(None, "slab", None, None), P(), P(), P()),
        check_vma=False,
    )
```

time: 617 us -> 91.1 us (0.15)
  blocking collectives: 442 us -> 0 us
  Pallas kernels: 0 us -> 86.5 us
  starting transfers between devices: 68.7 us -> 0 us
  waiting for transfers between devices: 66.6 us -> 0 us
  other arithmetic: 22.6 us -> 0 us
  local copies, waits for them, and re-layouts: 14.3 us -> 3.76 us
    psum x40 -> x0, blocking collectives: 442 us -> none  [one_axis_at_a_time(): value = lax.psum(value, axis)]
    pallas_call x0 -> x1, Pallas kernels: none -> 86.5 us  [shards(): pl.pallas_call(functools.partial(kernel, n, group), out_shape=(jax.ShapeD...]
    ppermute x22 -> x0, starting transfers between devices: 68.7 us -> none  [from_behind(): return lax.ppermute(block, axis, route)]
    ppermute x22 -> x0, waiting for transfers between devices: 66.6 us -> none  [from_behind(): return lax.ppermute(block, axis, route)]
    reduce_sum x11 -> x0, other arithmetic: 17.1 us -> none  [the longest x10 16.6 us: inner(): return jnp.sum(first * second, axis=(1, 2, 3))]
    slice x44 -> x0, local copies, waits for them, and re-layouts: 10.8 us -> none  [the longest x22 8.93 us: in_plane(): return beside + jnp.roll(field, 1, 3) + jnp.roll(field, -1, 3)]
  transfers between devices with their start and end apart: 22 -> 0, of which waited for: 18 -> 0; matrix products, arithmetic and copies ran while one was open for 5% -> 0% of each run, Pallas kernels for 0% -> 0%
where the time goes in v1:
time: 91.1 us; the launch traced here: 90.9 us
  Pallas kernels  86.5 us (95%)
  local copies, waits for them, and re-layouts  3.76 us (4%)
    pallas_call x1, Pallas kernels, shards(): pl.pallas_call(functools.partial(kernel, n, group), out_shape=(jax.ShapeD...  86.5 us
    unnamed x10, local copies, waits for them, and re-layouts  3.76 us

profile of v1, /device:TPU:1, one launch (start us, length us, event | category | flops | bytes accessed | tf_op | source)
XLA Modules:
  0.0 90.9 jit_solution(9959020619884550681)
XLA Ops:
  0.6 86.5 %shard_map.66 = (f32[2,1,256,256]{3,2,1,0:T(8,128)}, f32[2,8]{1,0:T(2,128)}, f32[2,7]{1,0:T(2,128)}, f32[2,6]{1,0:T(2,128)}) custom-call(f32[2,1,256,256]{3,2,1,0:T(8,128)} %sv_ref.1, s32[1,256,256]{2,1,0:T(8,128)} %lev_ref.1, f32[16]{0:T(128)} %en_ref.1), custom_call_target="tpu_custom_call" | custom-call | tf_op jit(solution)/shard_map/pallas_call | solution.py:451
  87.1 0.0 copy-start.2
  87.1 1.9 %copy.11 = f32[2,1,256,256]{3,2,1,0:T(8,128)} copy(f32[2,1,256,256]{3,2,1,0:T(8,128)} %get-tuple-element.8) | data formatting | bytes 1048576
  89.0 0.0 copy-done.2
  89.0 0.0 copy-start.1
  89.0 0.6 copy.12
  89.6 0.1 copy-done.1
  89.7 0.0 copy-start
  89.7 0.6 copy.13
  90.2 0.1 copy-done
  90.3 0.6 copy.14
Async XLA Ops:
  87.1 1.9 %copy-start.2 = (f32[2,8]{1,0:T(2,128)S(1)}, f32[2,8]{1,0:T(2,128)}, u32[]{:S(2)}) copy-start(f32[2,8]{1,0:T(2,128)} %get-tuple-element.9) | copy-start | bytes 196
  89.0 0.7 copy-start.1
  89.7 0.7 copy-start

commit v2 on v1

--- a/solution.py
+++ b/solution.py
@@ -8,7 +8,7 @@
 from jax.sharding import PartitionSpec as P
 
 STEPS = 8
-CHUNKS = 2
+CHUNKS = 4
 BLOCK = 32
 MESH = pl.DeviceIdType.MESH
 
@@ -103,16 +103,25 @@
     return diag, square
 
 
-def kernel(
+def scaling(en_ref):
+    energies = [en_ref[i] for i in range(en_ref.shape[0])]
+    shift = sum(energies[1:], energies[0]) * (1.0 / len(energies))
+    spread = sum((e - shift) * (e - shift) for e in energies) * (1.0 / len(energies))
+    return energies, shift, spread + 6.0
+
+
+def inverse_width(square, nx):
+    return 1.0 / jnp.sqrt(jnp.full((1, nx), square, jnp.float32))
+
+
+def iterate(
     n,
     group,
     sv_ref,
     lev_ref,
     en_ref,
-    field_ref,
-    diag_ref,
-    off_ref,
-    mom_ref,
+    row_ref,
+    kept_ref,
     basis,
     below,
     above,
@@ -123,8 +132,9 @@
     row_b,
     near,
     far,
-    table,
     load_sem,
+    keep_sem,
+    met,
     up_send,
     up_recv,
     down_send,
@@ -151,6 +161,13 @@
         place = lax.rem(team + k, groups)
         return place, place * group + mine
 
+    def tell(sem, device):
+        pl.semaphore_signal(sem, inc=1, device_id=(device,), device_id_type=MESH)
+
+    barrier = pltpu.get_barrier_semaphore()
+    tell(barrier, up)
+    tell(barrier, down)
+
     def load(v, c):
         part = pl.ds(c * rows, rows)
         return pltpu.make_async_copy(
@@ -163,16 +180,16 @@
             load(v, c).start()
     load_levels.start()
 
-    barrier = pltpu.get_barrier_semaphore()
-
-    def greet(device):
-        pl.semaphore_signal(barrier, inc=1, device_id=(device,), device_id_type=MESH)
-
-    greet(up)
-    greet(down)
-    lax.fori_loop(1, group, lambda k, _: greet(near_peer(k)[1]), None)
-    lax.fori_loop(1, groups, lambda k, _: greet(far_peer(k)[1]), None)
-    pl.semaphore_wait(barrier, group + groups)
+    pl.semaphore_wait(barrier, 2)
+
+    rounds = n.bit_length() - 2
+
+    def hear(r):
+        pl.semaphore_wait(met.at[r - 1], 2)
+
+    def say(r, distance):
+        tell(met.at[r - 1], lax.rem(me + distance, n))
+        tell(met.at[r - 1], lax.rem(me + n - distance, n))
 
     def halo(k, v, c, upward):
         part = pl.ds(c * rows, rows)
@@ -194,11 +211,8 @@
             halo(0, v, c, True).start()
             halo(0, v, c, False).start()
 
-    energies = [en_ref[i] for i in range(en_ref.shape[0])]
-    shift = sum(energies[1:], energies[0]) * (1.0 / len(energies))
-    spread = sum((e - shift) * (e - shift) for e in energies) * (1.0 / len(energies))
-    width_row = jnp.full((1, nx), spread + 6.0, jnp.float32)
-    inv_row = 1.0 / jnp.sqrt(width_row)
+    energies, shift, square = scaling(en_ref)
+    inv_row = inverse_width(square, nx)
 
     load_levels.wait()
 
@@ -291,9 +305,39 @@
             totals += [total[:2], total[2:]]
         gather(k, totals)
 
-    lax.fori_loop(0, STEPS - 2, lambda k, _: step(k), None)
-    step(STEPS - 2, final_sends=True)
-    step(STEPS - 1, last=True)
+    def keep(k):
+        return pltpu.make_async_copy(basis.at[k + 2], kept_ref.at[k], keep_sem.at[k])
+
+    say(1, 1)
+    step(0)
+    keep(0).start()
+
+    def middle(k, distance):
+        @pl.when(k <= rounds)
+        def _():
+            hear(k)
+
+        @pl.when(k < rounds)
+        def _():
+            say(k + 1, distance)
+
+        step(k)
+
+        @pl.when(k < 3)
+        def _():
+            keep(k).start()
+
+        return distance * 2
+
+    lax.fori_loop(1, STEPS - 2, middle, 2)
+    for k in (STEPS - 2, STEPS - 1):
+        if k <= rounds:
+            hear(k)
+        if k < rounds:
+            say(k + 1, 2**k)
+        step(k, final_sends=k == STEPS - 2, last=k == STEPS - 1)
+    if rounds == STEPS:
+        hear(rounds)
 
     packed = gathered[...]
     for shift_by in (4, 2, 1):
@@ -325,7 +369,52 @@
 
     row = exchange(packed[0:1], row_a, near, mine, near_peer, group, near_send, near_recv)
     row = exchange(row, row_b, far, team, far_peer, groups, far_send, far_recv)
-
+    row_ref[...] = row
+
+    def drain(k, _):
+        for v in range(2):
+            for c in range(CHUNKS):
+                halo(k, v, c, True).wait_send()
+                halo(k, v, c, False).wait_send()
+        return None
+
+    lax.fori_loop(0, STEPS - 1, drain, None)
+    for v in range(2):
+        for c in range(CHUNKS):
+            halo(STEPS - 1, v, c, c < CHUNKS // 2).wait_send()
+    for k in range(3):
+        keep(k).wait()
+
+
+def combine(
+    en_ref,
+    row_ref,
+    sv_ref,
+    kept_ref,
+    field_ref,
+    diag_ref,
+    off_ref,
+    mom_ref,
+    basis,
+    field,
+    table,
+    load_sem,
+    out_sem,
+):
+    ny, nx = field.shape[1:]
+
+    def load(v, k):
+        source = kept_ref.at[k - 1, v] if k else sv_ref.at[v, 0]
+        return pltpu.make_async_copy(source, basis.at[k, v], load_sem.at[v, k])
+
+    for v in range(2):
+        for k in range(4):
+            load(v, k).start()
+
+    _, shift, square = scaling(en_ref)
+    inv_row = inverse_width(square, 128)
+    row = row_ref[...]
+    row_lane = lax.broadcasted_iota(jnp.int32, (1, 128), 1)
     tall_row = lax.broadcasted_iota(jnp.int32, (32, 128), 0)
     tall_lane = lax.broadcasted_iota(jnp.int32, (32, 128), 1)
     spread_row = jnp.broadcast_to(row, (32, 128))
@@ -339,7 +428,7 @@
     crosses = [(table[8 + k : 9 + k, :], table[24 + k : 25 + k, :]) for k in range(STEPS)]
     diag, square = coefficients(norms, crosses)
 
-    width = 1.0 / inv_row[:, :128]
+    width = 1.0 / inv_row
     alphas = [shift + width * a[0] for a in diag]
     betas = [width * jnp.sqrt(b[0]) for b in square]
     zero = jnp.zeros((1, 128), jnp.float32)
@@ -406,35 +495,31 @@
         ref[0:1, :] = packed[:, : len(values)]
         ref[1:2, :] = pltpu.roll(packed, 64, 1)[:, : len(values)]
 
+    def store(v):
+        return pltpu.make_async_copy(field.at[v], field_ref.at[v, 0], out_sem.at[v])
+
     for v in range(2):
-        keep = row_lane < 64 if v == 0 else row_lane >= 64
-        scale = [jnp.where(keep, q, pltpu.roll(q, 64, 1)) for q in t3]
+        own = row_lane < 64 if v == 0 else row_lane >= 64
+        scale = [jnp.where(own, q, pltpu.roll(q, 64, 1)) for q in t3]
         scale = [jnp.concatenate([q, q], axis=1) for q in scale]
+        for k in range(4):
+            load(v, k).wait()
 
         def finish(b, _):
             part = pl.ds(pl.multiple_of(b * BLOCK, BLOCK), BLOCK)
-            value = scale[0] * basis[1, v, part, :] + scale[1] * basis[2, v, part, :]
-            value = value + scale[2] * basis[3, v, part, :]
-            field_ref[v, 0, part, :] = value + scale[3] * basis[4, v, part, :]
+            value = scale[0] * basis[0, v, part, :] + scale[1] * basis[1, v, part, :]
+            value = value + scale[2] * basis[2, v, part, :]
+            field[v, part, :] = value + scale[3] * basis[3, v, part, :]
             return None
 
         lax.fori_loop(0, ny // BLOCK, finish, None)
+        store(v).start()
 
     emit(diag_ref, alphas)
     emit(off_ref, betas)
     emit(mom_ref, moments)
-
-    def drain(k, _):
-        for v in range(2):
-            for c in range(CHUNKS):
-                halo(k, v, c, True).wait_send()
-                halo(k, v, c, False).wait_send()
-        return None
-
-    lax.fori_loop(0, STEPS - 1, drain, None)
     for v in range(2):
-        for c in range(CHUNKS):
-            halo(STEPS - 1, v, c, c < CHUNKS // 2).wait_send()
+        store(v).wait()
 
 
 def solution(mesh):
@@ -448,16 +533,16 @@
         vmem = pl.BlockSpec(memory_space=pltpu.VMEM)
         hbm = pl.BlockSpec(memory_space=pl.ANY)
         halo_sem = dma((STEPS, vecs, CHUNKS))
-        return pl.pallas_call(
-            functools.partial(kernel, n, group),
+        smem = pl.BlockSpec(memory_space=pltpu.SMEM)
+        groups = n // group
+        row, kept = pl.pallas_call(
+            functools.partial(iterate, n, group),
             out_shape=(
-                jax.ShapeDtypeStruct(start_vectors.shape, f32),
-                jax.ShapeDtypeStruct((vecs, STEPS), f32),
-                jax.ShapeDtypeStruct((vecs, STEPS - 1), f32),
-                jax.ShapeDtypeStruct((vecs, 6), f32),
+                jax.ShapeDtypeStruct((1, 128), f32),
+                jax.ShapeDtypeStruct((3, vecs, ny, nx), f32),
             ),
-            in_specs=[hbm, hbm, pl.BlockSpec(memory_space=pltpu.SMEM)],
-            out_specs=(vmem, vmem, vmem, vmem),
+            in_specs=[hbm, hbm, smem],
+            out_specs=(vmem, hbm),
             scratch_shapes=[
                 pltpu.VMEM((STEPS + 1, vecs, ny, nx), f32),
                 pltpu.VMEM((STEPS, vecs, ny, nx), f32),
@@ -468,20 +553,39 @@
                 pltpu.VMEM((1, 128), f32),
                 pltpu.VMEM((1, 128), f32),
                 pltpu.VMEM((group, 1, 128), f32),
-                pltpu.VMEM((n // group, 1, 128), f32),
-                pltpu.VMEM((32, 128), f32),
+                pltpu.VMEM((groups, 1, 128), f32),
                 dma((2 * CHUNKS + 1,)),
+                dma((3,)),
+                pltpu.SemaphoreType.REGULAR((STEPS,)),
                 halo_sem,
                 halo_sem,
                 halo_sem,
                 halo_sem,
                 dma((group,)),
                 dma((group,)),
-                dma((n // group,)),
-                dma((n // group,)),
+                dma((groups,)),
+                dma((groups,)),
             ],
             compiler_params=pltpu.CompilerParams(collective_id=0, has_side_effects=True),
         )(start_vectors, levels, energies)
+        return pl.pallas_call(
+            combine,
+            out_shape=(
+                jax.ShapeDtypeStruct(start_vectors.shape, f32),
+                jax.ShapeDtypeStruct((vecs, STEPS), f32),
+                jax.ShapeDtypeStruct((vecs, STEPS - 1), f32),
+                jax.ShapeDtypeStruct((vecs, 6), f32),
+            ),
+            in_specs=[smem, vmem, hbm, hbm],
+            out_specs=(hbm, vmem, vmem, vmem),
+            scratch_shapes=[
+                pltpu.VMEM((4, vecs, ny, nx), f32),
+                pltpu.VMEM((vecs, ny, nx), f32),
+                pltpu.VMEM((32, 128), f32),
+                dma((vecs, 4)),
+                dma((vecs,)),
+            ],
+        )(energies, row, start_vectors, kept)
 
     return jax.shard_map(
         shards,

time: 91.1 us -> 83.2 us (0.913)
  Pallas kernels: 86.5 us -> 82.4 us
  local copies, waits for them, and re-layouts: 3.76 us -> 0 us
    pallas_call x1 -> x2, Pallas kernels: 86.5 us -> 82.4 us  [the longest x1 78.7 us: shards(): pl.pallas_call(functools.partial(iterate, n, group), out_shape=(jax.Shape...]
    unnamed x10 -> x0, local copies, waits for them, and re-layouts: 3.76 us -> none
where the time goes in v2:
time: 83.2 us; the launch traced here: 83 us
  Pallas kernels  82.4 us (99%)
    pallas_call x1, Pallas kernels, shards(): pl.pallas_call(functools.partial(iterate, n, group), out_shape=(jax.Shape...  78.7 us
    pallas_call x1, Pallas kernels, shards(): pl.pallas_call(combine, out_shape=(jax.ShapeDtypeStruct(start_vectors.sha...  3.69 us

profile of v2, /device:TPU:1, one launch (start us, length us, event | category | flops | bytes accessed | tf_op | source)
XLA Modules:
  0.0 83.0 jit_solution(16599088989059545949)
XLA Ops:
  0.6 78.7 %shard_map.66 = (f32[1,128]{1,0:T(1,128)}, f32[3,2,256,256]{3,2,1,0:T(8,128)}) custom-call(f32[2,1,256,256]{3,2,1,0:T(8,128)} %sv_ref.3, s32[1,256,256]{2,1,0:T(8,128)} %lev_ref.1, f32[16]{0:T(128)} %en_ref.3), custom_call_target="tpu_custom_call" | custom-call | tf_op jit(solution)/shard_map/pallas_call | solution.py:538
  79.3 3.7 %shard_map.67 = (f32[2,1,256,256]{3,2,1,0:T(8,128)}, f32[2,8]{1,0:T(2,128)}, f32[2,7]{1,0:T(2,128)}, f32[2,6]{1,0:T(2,128)}) custom-call(f32[16]{0:T(128)} %en_ref.3, f32[1,128]{1,0:T(1,128)} %get-tuple-element.6.row_ref, f32[2,1,256,256]{3,2,1,0:T(8,128)} %sv_ref.3, f32[3,2,256,256]{3,2,1,0:T(8,128)} %get-tuple-element.7.kept_ref), custom_call_target="tpu_custom_call" | custom-call | tf_op jit(solution)/shard_map/pallas_call | solution.py:571

commit v3 on v2

--- a/solution.py
+++ b/solution.py
@@ -121,19 +121,17 @@
     lev_ref,
     en_ref,
     row_ref,
-    kept_ref,
     basis,
     below,
     above,
     onsite,
     levels,
-    gathered,
+    stats,
     row_a,
     row_b,
     near,
     far,
     load_sem,
-    keep_sem,
     met,
     up_send,
     up_recv,
@@ -146,6 +144,7 @@
 ):
     ny, nx = onsite.shape
     rows = ny // CHUNKS
+    block_rows = min(BLOCK, rows // 2)
     groups = n // group
     me = lax.axis_index("slab")
     up = lax.rem(me + 1, n)
@@ -153,13 +152,20 @@
     mine = lax.rem(me, group)
     team = me // group
 
-    def near_peer(k):
-        place = lax.rem(mine + k, group)
-        return place, team * group + place
-
-    def far_peer(k):
-        place = lax.rem(team + k, groups)
-        return place, place * group + mine
+    def ring(d, size):
+        return min(d, size - d)
+
+    near_peers = []
+    for d in sorted(range(1, group), key=lambda d: -ring(d, group)):
+        place = lax.rem(mine + d, group)
+        near_peers.append((place, team * group + place))
+    long = min(8, groups)
+    wide = groups // long
+    far_peers = []
+    steps = [(a, b) for a in range(wide) for b in range(long) if (a, b) != (0, 0)]
+    for a, b in sorted(steps, key=lambda ab: -ring(ab[0], wide) - ring(ab[1], long)):
+        place = lax.rem(team // long + a, wide) * long + lax.rem(team + b, long)
+        far_peers.append((place, place * group + mine))
 
     def tell(sem, device):
         pl.semaphore_signal(sem, inc=1, device_id=(device,), device_id_type=MESH)
@@ -191,8 +197,10 @@
         tell(met.at[r - 1], lax.rem(me + distance, n))
         tell(met.at[r - 1], lax.rem(me + n - distance, n))
 
-    def halo(k, v, c, upward):
+    def halo(k, v, c, upward, half=False):
         part = pl.ds(c * rows, rows)
+        if half:
+            part = pl.ds(c * rows + (0 if upward else rows // 2), rows // 2)
         landing, send, recv, device = (
             (below, up_send, up_recv, up) if upward else (above, down_send, down_recv, down)
         )
@@ -216,101 +224,128 @@
 
     load_levels.wait()
 
-    def place_onsite(b, _):
-        part = pl.ds(pl.multiple_of(b * BLOCK, BLOCK), BLOCK)
+    def fold(x):
+        parts = [x[i : i + 8] for i in range(0, x.shape[0], 8)]
+        while len(parts) > 1:
+            parts = [a + b for a, b in zip(parts[::2], parts[1::2])]
+        return parts[0]
+
+    def place_onsite(b, carry):
+        part = pl.ds(pl.multiple_of(b * block_rows, block_rows), block_rows)
         ids = levels[part, :]
-        value = jnp.full((BLOCK, nx), energies[0], jnp.float32)
+        value = jnp.full((block_rows, nx), energies[0], jnp.float32)
         for i in range(1, len(energies)):
             value = jnp.where(ids == i, energies[i], value)
         onsite[part, :] = (value - shift) * inv_row
+        out = []
         for v in range(2):
-            basis[0, v, part, :] = jnp.zeros((BLOCK, nx), jnp.float32)
-        return None
-
-    lax.fori_loop(0, ny // BLOCK, place_onsite, None)
-    gathered[...] = jnp.zeros((8, 128), jnp.float32)
-
-    def fold(x):
-        x = (x[0:8] + x[8:16]) + (x[16:24] + x[24:32])
-        return x
-
-    def sweep(k, v, c, totals, last):
+            basis[0, v, part, :] = jnp.zeros((block_rows, nx), jnp.float32)
+            here = basis[1, v, part, :]
+            h, e = two_sum(carry[v][0], fold(here * here))
+            out.append((h, carry[v][1] + e))
+        return tuple(out)
+
+    def squeeze(total):
+        h, l = total
+        h, e = two_sum(h[:, :128], h[:, 128:])
+        return h, (l[:, :128] + l[:, 128:]) + e
+
+    zero_rows = jnp.zeros((8, nx), jnp.float32)
+    none = (zero_rows, zero_rows)
+    first_norms = lax.fori_loop(0, ny // block_rows, place_onsite, (none, none))
+    for v in range(2):
+        stats[4 * STEPS - 4 + v, 0], stats[4 * STEPS - 4 + v, 1] = squeeze(first_norms[v])
+
+    def sweep(k, v, first, count, totals, landed=None):
         def block(b, carry):
-            nh, nl, ch, cl = carry
-            start = pl.multiple_of(c * rows + b * BLOCK, BLOCK)
-            part = pl.ds(start, BLOCK)
+            start = pl.multiple_of(first + b * block_rows, block_rows)
+            part = pl.ds(start, block_rows)
             before = pl.ds(pl.multiple_of(lax.rem(start + (ny - 8), ny), 8), 8)
-            after = pl.ds(pl.multiple_of(lax.rem(start + BLOCK, ny), 8), 8)
+            after = pl.ds(pl.multiple_of(lax.rem(start + block_rows, ny), 8), 8)
             here = basis[k + 1, v, part, :]
             tall = jnp.concatenate(
                 [basis[k + 1, v, before, :], here, basis[k + 1, v, after, :]], axis=0
             )
-            height = BLOCK + 16
-            beside = pltpu.roll(tall, 1, 0)[8 : 8 + BLOCK]
-            beside = beside + pltpu.roll(tall, height - 1, 0)[8 : 8 + BLOCK]
+            height = block_rows + 16
+            beside = pltpu.roll(tall, 1, 0)[8 : 8 + block_rows]
+            beside = beside + pltpu.roll(tall, height - 1, 0)[8 : 8 + block_rows]
             beside = beside + (pltpu.roll(here, 1, 1) + pltpu.roll(here, nx - 1, 1))
-            if last:
-                one = (below if c < CHUNKS // 2 else above)[k, v, part, :]
+            if landed is not None:
+                one = landed[k, v, part, :]
                 beside = beside + (one + one)
             else:
                 beside = beside + (below[k, v, part, :] + above[k, v, part, :])
             new = onsite[part, :] * here - inv_row * beside
-            if not last:
+            out = []
+            if landed is None:
                 new = new - basis[k, v, part, :]
                 basis[k + 2, v, part, :] = new
-            nh, e = two_sum(nh, fold(here * here))
-            ch, d = two_sum(ch, fold(new * here))
-            return nh, nl + e, ch, cl + d
-
-        return lax.fori_loop(0, rows // BLOCK, block, totals)
+                out.append(new * new)
+            out.append(new * here)
+            added = []
+            for (h, l), x in zip(carry, out):
+                h, e = two_sum(h, fold(x))
+                added.append((h, l + e))
+            return tuple(added)
+
+        return lax.fori_loop(0, count // block_rows, block, totals)
 
     sub = lax.broadcasted_iota(jnp.int32, (8, 128), 0)
     lane = lax.broadcasted_iota(jnp.int32, (8, 128), 1)
 
-    def gather(k, totals):
+    def lane_sums(items):
         high = jnp.zeros((8, 128), jnp.float32)
         low = jnp.zeros((8, 128), jnp.float32)
-        for q, (h, l) in enumerate(totals):
-            h, e = two_sum(h[:, :128], h[:, 128:])
-            l = (l[:, :128] + l[:, 128:]) + e
+        target = jnp.full((8, 128), 1000, jnp.int32)
+        for q, (h, l, place) in enumerate(items):
             for shift_by in (4, 2, 1):
                 h, e = two_sum(h, pltpu.roll(h, shift_by, 0))
                 l = l + pltpu.roll(l, shift_by, 0) + e
             high = jnp.where(sub == q, h, high)
             low = jnp.where(sub == q, l, low)
+            target = jnp.where(sub == q, place, target)
         for shift_by in (64, 32, 16, 8, 4, 2, 1):
             high, e = two_sum(high, pltpu.roll(high, shift_by, 1))
             low = low + pltpu.roll(low, shift_by, 1) + e
-        target = jnp.where(sub < 4, (sub // 2) * 64 + lax.rem(sub, 2) * 8 + k, 1000)
-        gathered[...] += jnp.where(lane == target, high, 0.0) + jnp.where(
+        return jnp.where(lane == target, high, 0.0) + jnp.where(
             lane == target + 16, low, 0.0
         )
 
-    def step(k, final_sends=False, last=False):
-        totals = []
+    def step(k, final_sends=False):
         for v in range(2):
-            zero = jnp.zeros((8, nx), jnp.float32)
-            total = (zero, zero, zero, zero)
+            totals = (none, none)
             for c in range(CHUNKS):
-                if not last or c < CHUNKS // 2:
-                    halo(k, v, c, True).wait_recv()
-                if not last or c >= CHUNKS // 2:
-                    halo(k, v, c, False).wait_recv()
-                total = sweep(k, v, c, total, last)
-                if not last:
-                    if not final_sends or c < CHUNKS // 2:
-                        halo(k + 1, v, c, True).start()
-                    if not final_sends or c >= CHUNKS // 2:
-                        halo(k + 1, v, c, False).start()
-            totals += [total[:2], total[2:]]
-        gather(k, totals)
-
-    def keep(k):
-        return pltpu.make_async_copy(basis.at[k + 2], kept_ref.at[k], keep_sem.at[k])
+                halo(k, v, c, True).wait_recv()
+                halo(k, v, c, False).wait_recv()
+                totals = sweep(k, v, c * rows, rows, totals)
+                halo(k + 1, v, c, True, final_sends).start()
+                halo(k + 1, v, c, False, final_sends).start()
+            for q in range(2):
+                stats[4 * k + 2 * v + q, 0], stats[4 * k + 2 * v + q, 1] = squeeze(totals[q])
+
+    def last_step():
+        k = STEPS - 1
+        ends = []
+        for v in range(2):
+            totals = (none,)
+            for c in range(CHUNKS):
+                if v == 1 and c == CHUNKS - 1:
+                    places = [64 * (i % 4 // 2) + (8 + i // 4 if i % 2 else 1 + i // 4) for i in range(4 * k)]
+                    places += [0, 64]
+                    packed = jnp.zeros((8, 128), jnp.float32)
+                    for i in range(0, len(places), 8):
+                        packed = packed + lane_sums(
+                            [(stats[j, 0], stats[j, 1], places[j]) for j in range(i, min(i + 8, len(places)))]
+                        )
+                halo(k, v, c, True, True).wait_recv()
+                halo(k, v, c, False, True).wait_recv()
+                totals = sweep(k, v, c * rows, rows // 2, totals, below)
+                totals = sweep(k, v, c * rows + rows // 2, rows // 2, totals, above)
+            ends.append(squeeze(totals[0]))
+        return packed + lane_sums([(h, l, 64 * v + 8 + k) for v, (h, l) in enumerate(ends)])
 
     say(1, 1)
     step(0)
-    keep(0).start()
 
     def middle(k, distance):
         @pl.when(k <= rounds)
@@ -322,11 +357,6 @@
             say(k + 1, distance)
 
         step(k)
-
-        @pl.when(k < 3)
-        def _():
-            keep(k).start()
-
         return distance * 2
 
     lax.fori_loop(1, STEPS - 2, middle, 2)
@@ -335,41 +365,47 @@
             hear(k)
         if k < rounds:
             say(k + 1, 2**k)
-        step(k, final_sends=k == STEPS - 2, last=k == STEPS - 1)
+        if k == STEPS - 2:
+            step(k, final_sends=True)
+    packed = last_step()
     if rounds == STEPS:
         hear(rounds)
 
-    packed = gathered[...]
     for shift_by in (4, 2, 1):
         packed = packed + pltpu.roll(packed, shift_by, 0)
 
     row_lane = lax.broadcasted_iota(jnp.int32, (1, 128), 1)
     is_high = lax.rem(row_lane, 64) < 16
 
-    def exchange(row, staging, slots, place, peer, count, send, recv):
-        def copy(k, arriving):
-            other, device = peer(k)
-            slot = other if arriving else place
+    def exchange(row, staging, slots, place, peers, send, recv):
+        def copy(i, slot):
             return pltpu.make_async_remote_copy(
                 src_ref=staging,
                 dst_ref=slots.at[slot],
-                send_sem=send.at[k],
+                send_sem=send.at[i],
                 recv_sem=recv.at[slot],
-                device_id=(device,),
+                device_id=(peers[i][1],),
                 device_id_type=MESH,
             )
 
         staging[...] = row
         slots[place] = row
-        lax.fori_loop(1, count, lambda k, _: copy(k, False).start(), None)
-        lax.fori_loop(1, count, lambda k, _: copy(k, True).wait_recv(), None)
-        total, lost = tree_rows([slots[i] for i in range(count)])
-        lax.fori_loop(1, count, lambda k, _: copy(k, False).wait_send(), None)
-        return jnp.where(is_high, total, total + pltpu.roll(lost, 16, 1))
-
-    row = exchange(packed[0:1], row_a, near, mine, near_peer, group, near_send, near_recv)
-    row = exchange(row, row_b, far, team, far_peer, groups, far_send, far_recv)
+        for i in range(len(peers)):
+            copy(i, place).start()
+        for i in reversed(range(len(peers))):
+            copy(i, peers[i][0]).wait_recv()
+        total, lost = tree_rows([slots[i] for i in range(len(peers) + 1)])
+        return jnp.where(is_high, total, total + pltpu.roll(lost, 16, 1)), [
+            copy(i, place) for i in range(len(peers))
+        ]
+
+    row, sent = exchange(packed[0:1], row_a, near, mine, near_peers, near_send, near_recv)
+    row, more = exchange(row, row_b, far, team, far_peers, far_send, far_recv)
+    row = jnp.where(row_lane == 40, shift, row)
+    row = jnp.where(row_lane == 41, inv_row[:, :128], row)
     row_ref[...] = row
+    for copy in sent + more:
+        copy.wait_send()
 
     def drain(k, _):
         for v in range(2):
@@ -381,40 +417,27 @@
     lax.fori_loop(0, STEPS - 1, drain, None)
     for v in range(2):
         for c in range(CHUNKS):
-            halo(STEPS - 1, v, c, c < CHUNKS // 2).wait_send()
-    for k in range(3):
-        keep(k).wait()
+            halo(STEPS - 1, v, c, True, True).wait_send()
+            halo(STEPS - 1, v, c, False, True).wait_send()
 
 
 def combine(
-    en_ref,
     row_ref,
-    sv_ref,
-    kept_ref,
+    basis,
     field_ref,
     diag_ref,
     off_ref,
     mom_ref,
-    basis,
     field,
     table,
-    load_sem,
     out_sem,
 ):
     ny, nx = field.shape[1:]
 
-    def load(v, k):
-        source = kept_ref.at[k - 1, v] if k else sv_ref.at[v, 0]
-        return pltpu.make_async_copy(source, basis.at[k, v], load_sem.at[v, k])
-
-    for v in range(2):
-        for k in range(4):
-            load(v, k).start()
-
-    _, shift, square = scaling(en_ref)
-    inv_row = inverse_width(square, 128)
     row = row_ref[...]
     row_lane = lax.broadcasted_iota(jnp.int32, (1, 128), 1)
+    shift = jnp.sum(jnp.where(row_lane == 40, row, 0.0), axis=1, keepdims=True)
+    inv_row = jnp.sum(jnp.where(row_lane == 41, row, 0.0), axis=1, keepdims=True)
     tall_row = lax.broadcasted_iota(jnp.int32, (32, 128), 0)
     tall_lane = lax.broadcasted_iota(jnp.int32, (32, 128), 1)
     spread_row = jnp.broadcast_to(row, (32, 128))
@@ -428,7 +451,7 @@
     crosses = [(table[8 + k : 9 + k, :], table[24 + k : 25 + k, :]) for k in range(STEPS)]
     diag, square = coefficients(norms, crosses)
 
-    width = 1.0 / inv_row
+    width = jnp.broadcast_to(1.0 / inv_row, (1, 128))
     alphas = [shift + width * a[0] for a in diag]
     betas = [width * jnp.sqrt(b[0]) for b in square]
     zero = jnp.zeros((1, 128), jnp.float32)
@@ -495,31 +518,36 @@
         ref[0:1, :] = packed[:, : len(values)]
         ref[1:2, :] = pltpu.roll(packed, 64, 1)[:, : len(values)]
 
-    def store(v):
-        return pltpu.make_async_copy(field.at[v], field_ref.at[v, 0], out_sem.at[v])
+    half = ny // 2
+
+    def store(v, i):
+        part = pl.ds(i * half, half)
+        return pltpu.make_async_copy(
+            field.at[v, part], field_ref.at[v, 0, part], out_sem.at[v, i]
+        )
 
     for v in range(2):
         own = row_lane < 64 if v == 0 else row_lane >= 64
         scale = [jnp.where(own, q, pltpu.roll(q, 64, 1)) for q in t3]
         scale = [jnp.concatenate([q, q], axis=1) for q in scale]
-        for k in range(4):
-            load(v, k).wait()
-
-        def finish(b, _):
-            part = pl.ds(pl.multiple_of(b * BLOCK, BLOCK), BLOCK)
-            value = scale[0] * basis[0, v, part, :] + scale[1] * basis[1, v, part, :]
-            value = value + scale[2] * basis[2, v, part, :]
-            field[v, part, :] = value + scale[3] * basis[3, v, part, :]
-            return None
-
-        lax.fori_loop(0, ny // BLOCK, finish, None)
-        store(v).start()
+        for i in range(2):
+
+            def finish(b, _):
+                part = pl.ds(pl.multiple_of(i * half + b * BLOCK, BLOCK), BLOCK)
+                value = scale[0] * basis[1, v, part, :] + scale[1] * basis[2, v, part, :]
+                value = value + scale[2] * basis[3, v, part, :]
+                field[v, part, :] = value + scale[3] * basis[4, v, part, :]
+                return None
+
+            lax.fori_loop(0, half // BLOCK, finish, None)
+            store(v, i).start()
 
     emit(diag_ref, alphas)
     emit(off_ref, betas)
     emit(mom_ref, moments)
     for v in range(2):
-        store(v).wait()
+        for i in range(2):
+            store(v, i).wait()
 
 
 def solution(mesh):
@@ -531,31 +559,29 @@
         f32 = jnp.float32
         dma = pltpu.SemaphoreType.DMA
         vmem = pl.BlockSpec(memory_space=pltpu.VMEM)
-        hbm = pl.BlockSpec(memory_space=pl.ANY)
+        hbm = pl.BlockSpec(memory_space=pltpu.HBM)
         halo_sem = dma((STEPS, vecs, CHUNKS))
         smem = pl.BlockSpec(memory_space=pltpu.SMEM)
         groups = n // group
-        row, kept = pl.pallas_call(
+        row, basis = pl.pallas_call(
             functools.partial(iterate, n, group),
             out_shape=(
-                jax.ShapeDtypeStruct((1, 128), f32),
-                jax.ShapeDtypeStruct((3, vecs, ny, nx), f32),
+                pltpu.VMEM((1, 128), f32),
+                pltpu.VMEM((STEPS + 1, vecs, ny, nx), f32),
             ),
             in_specs=[hbm, hbm, smem],
-            out_specs=(vmem, hbm),
+            out_specs=(vmem, vmem),
             scratch_shapes=[
-                pltpu.VMEM((STEPS + 1, vecs, ny, nx), f32),
                 pltpu.VMEM((STEPS, vecs, ny, nx), f32),
                 pltpu.VMEM((STEPS, vecs, ny, nx), f32),
                 pltpu.VMEM((ny, nx), f32),
                 pltpu.VMEM((ny, nx), jnp.int32),
-                pltpu.VMEM((8, 128), f32),
+                pltpu.VMEM((4 * STEPS - 2, 2, 8, 128), f32),
                 pltpu.VMEM((1, 128), f32),
                 pltpu.VMEM((1, 128), f32),
                 pltpu.VMEM((group, 1, 128), f32),
                 pltpu.VMEM((groups, 1, 128), f32),
                 dma((2 * CHUNKS + 1,)),
-                dma((3,)),
                 pltpu.SemaphoreType.REGULAR((STEPS,)),
                 halo_sem,
                 halo_sem,
@@ -566,7 +592,9 @@
                 dma((groups,)),
                 dma((groups,)),
             ],
-            compiler_params=pltpu.CompilerParams(collective_id=0, has_side_effects=True),
+            compiler_params=pltpu.CompilerParams(
+                collective_id=0, has_side_effects=True, vmem_limit_bytes=62_000_000
+            ),
         )(start_vectors, levels, energies)
         return pl.pallas_call(
             combine,
@@ -576,16 +604,15 @@
                 jax.ShapeDtypeStruct((vecs, STEPS - 1), f32),
                 jax.ShapeDtypeStruct((vecs, 6), f32),
             ),
-            in_specs=[smem, vmem, hbm, hbm],
+            in_specs=[vmem, vmem],
             out_specs=(hbm, vmem, vmem, vmem),
             scratch_shapes=[
-                pltpu.VMEM((4, vecs, ny, nx), f32),
                 pltpu.VMEM((vecs, ny, nx), f32),
                 pltpu.VMEM((32, 128), f32),
-                dma((vecs, 4)),
-                dma((vecs,)),
+                dma((vecs, 2)),
             ],
-        )(energies, row, start_vectors, kept)
+            compiler_params=pltpu.CompilerParams(vmem_limit_bytes=8 * 2**20),
+        )(row, basis)
 
     return jax.shard_map(
         shards,

time: 83.2 us -> 80.1 us (0.963)
  Pallas kernels: 82.4 us -> 79.3 us
    pallas_call x1, Pallas kernels: 78.7 us -> 77 us  [shards(): pl.pallas_call(functools.partial(iterate, n, group), out_shape=(pltpu.VME...]
    pallas_call x1, Pallas kernels: 3.69 us -> 2.3 us  [shards(): pl.pallas_call(combine, out_shape=(jax.ShapeDtypeStruct(start_vectors.sha...]
where the time goes in v3:
time: 80.1 us; the launch traced here: 80 us
  Pallas kernels  79.3 us (99%)
    pallas_call x1, Pallas kernels, shards(): pl.pallas_call(functools.partial(iterate, n, group), out_shape=(pltpu.VME...  77 us
    pallas_call x1, Pallas kernels, shards(): pl.pallas_call(combine, out_shape=(jax.ShapeDtypeStruct(start_vectors.sha...  2.3 us

profile of v3, /device:TPU:1, one launch (start us, length us, event | category | flops | bytes accessed | tf_op | source)
XLA Modules:
  0.0 80.0 jit_solution(2202489360338294377)
XLA Ops:
  0.6 77.0 %shard_map.66 = (f32[1,128]{1,0:T(1,128)S(1)}, f32[9,2,256,256]{3,2,1,0:T(8,128)S(1)}) custom-call(f32[2,1,256,256]{3,2,1,0:T(8,128)} %sv_ref.1, s32[1,256,256]{2,1,0:T(8,128)} %lev_ref.1, f32[16]{0:T(128)} %en_ref.1), custom_call_target="tpu_custom_call" | custom-call | tf_op jit(solution)/shard_map/pallas_call | solution.py:566
  77.6 2.3 %shard_map.67 = (f32[2,1,256,256]{3,2,1,0:T(8,128)}, f32[2,8]{1,0:T(2,128)}, f32[2,7]{1,0:T(2,128)}, f32[2,6]{1,0:T(2,128)}) custom-call(f32[1,128]{1,0:T(1,128)S(1)} %get-tuple-element.6.row_ref, f32[9,2,256,256]{3,2,1,0:T(8,128)S(1)} %get-tuple-element.7.basis), custom_call_target="tpu_custom_call" | custom-call | tf_op jit(solution)/shard_map/pallas_call | solution.py:599

commit v4 on v3

--- a/solution.py
+++ b/solution.py
@@ -377,7 +377,21 @@
     row_lane = lax.broadcasted_iota(jnp.int32, (1, 128), 1)
     is_high = lax.rem(row_lane, 64) < 16
 
-    def exchange(row, staging, slots, place, peers, send, recv):
+    def drain(k, _):
+        for v in range(2):
+            for c in range(CHUNKS):
+                halo(k, v, c, True).wait_send()
+                halo(k, v, c, False).wait_send()
+        return None
+
+    def drain_all():
+        lax.fori_loop(0, STEPS - 1, drain, None)
+        for v in range(2):
+            for c in range(CHUNKS):
+                halo(STEPS - 1, v, c, True, True).wait_send()
+                halo(STEPS - 1, v, c, False, True).wait_send()
+
+    def exchange(row, staging, slots, place, peers, send, recv, meanwhile):
         def copy(i, slot):
             return pltpu.make_async_remote_copy(
                 src_ref=staging,
@@ -392,6 +406,7 @@
         slots[place] = row
         for i in range(len(peers)):
             copy(i, place).start()
+        meanwhile()
         for i in reversed(range(len(peers))):
             copy(i, peers[i][0]).wait_recv()
         total, lost = tree_rows([slots[i] for i in range(len(peers) + 1)])
@@ -399,26 +414,20 @@
             copy(i, place) for i in range(len(peers))
         ]
 
-    row, sent = exchange(packed[0:1], row_a, near, mine, near_peers, near_send, near_recv)
-    row, more = exchange(row, row_b, far, team, far_peers, far_send, far_recv)
+    row, sent = exchange(packed[0:1], row_a, near, mine, near_peers, near_send, near_recv, drain_all)
+
+    def drain_near():
+        for copy in sent:
+            copy.wait_send()
+
+    row, more = exchange(
+        row, row_b, far, team, far_peers, far_send, far_recv, drain_near
+    )
     row = jnp.where(row_lane == 40, shift, row)
     row = jnp.where(row_lane == 41, inv_row[:, :128], row)
     row_ref[...] = row
-    for copy in sent + more:
+    for copy in more:
         copy.wait_send()
-
-    def drain(k, _):
-        for v in range(2):
-            for c in range(CHUNKS):
-                halo(k, v, c, True).wait_send()
-                halo(k, v, c, False).wait_send()
-        return None
-
-    lax.fori_loop(0, STEPS - 1, drain, None)
-    for v in range(2):
-        for c in range(CHUNKS):
-            halo(STEPS - 1, v, c, True, True).wait_send()
-            halo(STEPS - 1, v, c, False, True).wait_send()
 
 
 def combine(
@@ -429,8 +438,12 @@
     off_ref,
     mom_ref,
     field,
+    diag_out,
+    off_out,
+    mom_out,
     table,
     out_sem,
+    small_sem,
 ):
     ny, nx = field.shape[1:]
 
@@ -518,7 +531,14 @@
         ref[0:1, :] = packed[:, : len(values)]
         ref[1:2, :] = pltpu.roll(packed, 64, 1)[:, : len(values)]
 
-    half = ny // 2
+    small = []
+    for k, (stage, ref, values) in enumerate(
+        [(diag_out, diag_ref, alphas), (off_out, off_ref, betas), (mom_out, mom_ref, moments)]
+    ):
+        emit(stage, values)
+        small.append(pltpu.make_async_copy(stage, ref, small_sem.at[k]))
+
+    half = ny // 4
 
     def store(v, i):
         part = pl.ds(i * half, half)
@@ -530,7 +550,7 @@
         own = row_lane < 64 if v == 0 else row_lane >= 64
         scale = [jnp.where(own, q, pltpu.roll(q, 64, 1)) for q in t3]
         scale = [jnp.concatenate([q, q], axis=1) for q in scale]
-        for i in range(2):
+        for i in range(4):
 
             def finish(b, _):
                 part = pl.ds(pl.multiple_of(i * half + b * BLOCK, BLOCK), BLOCK)
@@ -541,13 +561,15 @@
 
             lax.fori_loop(0, half // BLOCK, finish, None)
             store(v, i).start()
-
-    emit(diag_ref, alphas)
-    emit(off_ref, betas)
-    emit(mom_ref, moments)
+        if v == 0:
+            for copy in small:
+                copy.start()
+
     for v in range(2):
-        for i in range(2):
+        for i in range(4):
             store(v, i).wait()
+    for copy in small:
+        copy.wait()
 
 
 def solution(mesh):
@@ -605,11 +627,15 @@
                 jax.ShapeDtypeStruct((vecs, 6), f32),
             ),
             in_specs=[vmem, vmem],
-            out_specs=(hbm, vmem, vmem, vmem),
+            out_specs=(hbm, hbm, hbm, hbm),
             scratch_shapes=[
                 pltpu.VMEM((vecs, ny, nx), f32),
+                pltpu.VMEM((vecs, STEPS), f32),
+                pltpu.VMEM((vecs, STEPS - 1), f32),
+                pltpu.VMEM((vecs, 6), f32),
                 pltpu.VMEM((32, 128), f32),
-                dma((vecs, 2)),
+                dma((vecs, 4)),
+                dma((3,)),
             ],
             compiler_params=pltpu.CompilerParams(vmem_limit_bytes=8 * 2**20),
         )(row, basis)

time: 80.1 us -> 79.4 us (level)
  no operation moved by 1% of the time
where the time goes in v4:
time: 79.4 us; the launch traced here: 79.3 us
  Pallas kernels  78.6 us (99%)
    pallas_call x1, Pallas kernels, shards(): pl.pallas_call(functools.partial(iterate, n, group), out_shape=(pltpu.VME...  76.8 us
    pallas_call x1, Pallas kernels, shards(): pl.pallas_call(combine, out_shape=(jax.ShapeDtypeStruct(start_vectors.sha...  1.83 us

profile of v4, /device:TPU:1, one launch (start us, length us, event | category | flops | bytes accessed | tf_op | source)
XLA Modules:
  0.0 79.3 jit_solution(7165561621886514504)
XLA Ops:
  0.6 76.8 %shard_map.66 = (f32[1,128]{1,0:T(1,128)S(1)}, f32[9,2,256,256]{3,2,1,0:T(8,128)S(1)}) custom-call(f32[2,1,256,256]{3,2,1,0:T(8,128)} %sv_ref.1, s32[1,256,256]{2,1,0:T(8,128)} %lev_ref.1, f32[16]{0:T(128)} %en_ref.1), custom_call_target="tpu_custom_call" | custom-call | tf_op jit(solution)/shard_map/pallas_call | solution.py:588
  77.4 1.8 %shard_map.67 = (f32[2,1,256,256]{3,2,1,0:T(8,128)}, f32[2,8]{1,0:T(2,128)}, f32[2,7]{1,0:T(2,128)}, f32[2,6]{1,0:T(2,128)}) custom-call(f32[1,128]{1,0:T(1,128)S(1)} %get-tuple-element.6.row_ref, f32[9,2,256,256]{3,2,1,0:T(8,128)S(1)} %get-tuple-element.7.basis), custom_call_target="tpu_custom_call" | custom-call | tf_op jit(solution)/shard_map/pallas_call | solution.py:621

commit v5 on v4

--- a/solution.py
+++ b/solution.py
@@ -91,9 +91,18 @@
     for k in range(1, STEPS):
         new = {}
         for l in range(k, 2 * STEPS - k):
-            term = pair_sub(pair_add(old[l + 1], old[l - 1]), pair_mul(diag[-1], old[l]))
+            p, e = two_prod(diag[-1][0], old[l][0])
+            e = e + (diag[-1][0] * old[l][1] + diag[-1][1] * old[l][0])
+            sides, lost = two_sum(old[l + 1][0], old[l - 1][0])
+            lost = lost + (old[l + 1][1] + old[l - 1][1])
+            term, d = two_sum(sides, -p)
+            lost = (lost - e) + d
             if k > 1:
-                term = pair_sub(term, pair_mul(square[-1], older[l]))
+                p, e = two_prod(square[-1][0], older[l][0])
+                e = e + (square[-1][0] * older[l][1] + square[-1][1] * older[l][0])
+                term, d = two_sum(term, -p)
+                lost = (lost - e) + d
+            term = fast_two_sum(term, lost)
             new[l] = term
         square.append(pair_div(new[k], old[k - 1]))
         next_ratio = pair_div(new[k + 1], new[k])
@@ -132,6 +141,7 @@
     near,
     far,
     load_sem,
+    en_smem,
     met,
     up_send,
     up_recv,
@@ -185,6 +195,8 @@
         for c in range(CHUNKS):
             load(v, c).start()
     load_levels.start()
+    load_energies = pltpu.make_async_copy(en_ref, en_smem, load_sem.at[2 * CHUNKS + 1])
+    load_energies.start()
 
     pl.semaphore_wait(barrier, 2)
 
@@ -219,7 +231,8 @@
             halo(0, v, c, True).start()
             halo(0, v, c, False).start()
 
-    energies, shift, square = scaling(en_ref)
+    load_energies.wait()
+    energies, shift, square = scaling(en_smem)
     inv_row = inverse_width(square, nx)
 
     load_levels.wait()
@@ -583,7 +596,6 @@
         vmem = pl.BlockSpec(memory_space=pltpu.VMEM)
         hbm = pl.BlockSpec(memory_space=pltpu.HBM)
         halo_sem = dma((STEPS, vecs, CHUNKS))
-        smem = pl.BlockSpec(memory_space=pltpu.SMEM)
         groups = n // group
         row, basis = pl.pallas_call(
             functools.partial(iterate, n, group),
@@ -591,7 +603,7 @@
                 pltpu.VMEM((1, 128), f32),
                 pltpu.VMEM((STEPS + 1, vecs, ny, nx), f32),
             ),
-            in_specs=[hbm, hbm, smem],
+            in_specs=[hbm, hbm, hbm],
             out_specs=(vmem, vmem),
             scratch_shapes=[
                 pltpu.VMEM((STEPS, vecs, ny, nx), f32),
@@ -603,7 +615,8 @@
                 pltpu.VMEM((1, 128), f32),
                 pltpu.VMEM((group, 1, 128), f32),
                 pltpu.VMEM((groups, 1, 128), f32),
-                dma((2 * CHUNKS + 1,)),
+                dma((2 * CHUNKS + 2,)),
+                pltpu.SMEM(energies.shape, f32),
                 pltpu.SemaphoreType.REGULAR((STEPS,)),
                 halo_sem,
                 halo_sem,

time: 79.4 us -> 78.6 us (0.990)
  Pallas kernels: 78.6 us -> 77.8 us
where the time goes in v5:
time: 78.6 us; the launch traced here: 78.5 us
  Pallas kernels  77.8 us (99%)
    pallas_call x1, Pallas kernels, shards(): pl.pallas_call(functools.partial(iterate, n, group), out_shape=(pltpu.VME...  76.1 us
    pallas_call x1, Pallas kernels, shards(): pl.pallas_call(combine, out_shape=(jax.ShapeDtypeStruct(start_vectors.sha...  1.7 us

profile of v5, /device:TPU:1, one launch (start us, length us, event | category | flops | bytes accessed | tf_op | source)
XLA Modules:
  0.0 78.5 jit_solution(4132576445600926259)
XLA Ops:
  0.6 76.1 %shard_map.66 = (f32[1,128]{1,0:T(1,128)S(1)}, f32[9,2,256,256]{3,2,1,0:T(8,128)S(1)}) custom-call(f32[2,1,256,256]{3,2,1,0:T(8,128)} %sv_ref.1, s32[1,256,256]{2,1,0:T(8,128)} %lev_ref.1, f32[16]{0:T(128)} %en_ref.1), custom_call_target="tpu_custom_call" | custom-call | tf_op jit(solution)/shard_map/pallas_call | solution.py:600
  76.8 1.7 %shard_map.67 = (f32[2,1,256,256]{3,2,1,0:T(8,128)}, f32[2,8]{1,0:T(2,128)}, f32[2,7]{1,0:T(2,128)}, f32[2,6]{1,0:T(2,128)}) custom-call(f32[1,128]{1,0:T(1,128)S(1)} %get-tuple-element.6.row_ref, f32[9,2,256,256]{3,2,1,0:T(8,128)S(1)} %get-tuple-element.7.basis), custom_call_target="tpu_custom_call" | custom-call | tf_op jit(solution)/shard_map/pallas_call | solution.py:634

commit v6 on v5

--- a/solution.py
+++ b/solution.py
@@ -116,7 +116,7 @@
     energies = [en_ref[i] for i in range(en_ref.shape[0])]
     shift = sum(energies[1:], energies[0]) * (1.0 / len(energies))
     spread = sum((e - shift) * (e - shift) for e in energies) * (1.0 / len(energies))
-    return energies, shift, spread + 6.0
+    return energies, shift, spread + 9.0
 
 
 def inverse_width(square, nx):
@@ -427,14 +427,16 @@
             copy(i, place) for i in range(len(peers))
         ]
 
-    row, sent = exchange(packed[0:1], row_a, near, mine, near_peers, near_send, near_recv, drain_all)
-
-    def drain_near():
+    row, sent = exchange(
+        packed[0:1], row_b, far, team, far_peers, far_send, far_recv, drain_all
+    )
+
+    def drain_first():
         for copy in sent:
             copy.wait_send()
 
     row, more = exchange(
-        row, row_b, far, team, far_peers, far_send, far_recv, drain_near
+        row, row_a, near, mine, near_peers, near_send, near_recv, drain_first
     )
     row = jnp.where(row_lane == 40, shift, row)
     row = jnp.where(row_lane == 41, inv_row[:, :128], row)

time: 78.6 us -> 78.4 us (level)
  no operation moved by 1% of the time
where the time goes in v6:
time: 78.4 us; the launch traced here: 78.2 us
  Pallas kernels  77.6 us (99%)
    pallas_call x1, Pallas kernels, shards(): pl.pallas_call(functools.partial(iterate, n, group), out_shape=(pltpu.VME...  75.9 us
    pallas_call x1, Pallas kernels, shards(): pl.pallas_call(combine, out_shape=(jax.ShapeDtypeStruct(start_vectors.sha...  1.7 us

profile of v6, /device:TPU:1, one launch (start us, length us, event | category | flops | bytes accessed | tf_op | source)
XLA Modules:
  0.0 78.2 jit_solution(13342620913412689720)
XLA Ops:
  0.6 75.9 %shard_map.66 = (f32[1,128]{1,0:T(1,128)S(1)}, f32[9,2,256,256]{3,2,1,0:T(8,128)S(1)}) custom-call(f32[2,1,256,256]{3,2,1,0:T(8,128)} %sv_ref.1, s32[1,256,256]{2,1,0:T(8,128)} %lev_ref.1, f32[16]{0:T(128)} %en_ref.1), custom_call_target="tpu_custom_call" | custom-call | tf_op jit(solution)/shard_map/pallas_call | solution.py:602
  76.5 1.7 %shard_map.67 = (f32[2,1,256,256]{3,2,1,0:T(8,128)}, f32[2,8]{1,0:T(2,128)}, f32[2,7]{1,0:T(2,128)}, f32[2,6]{1,0:T(2,128)}) custom-call(f32[1,128]{1,0:T(1,128)S(1)} %get-tuple-element.6.row_ref, f32[9,2,256,256]{3,2,1,0:T(8,128)S(1)} %get-tuple-element.7.basis), custom_call_target="tpu_custom_call" | custom-call | tf_op jit(solution)/shard_map/pallas_call | solution.py:636

commit v7 on v6

--- a/solution.py
+++ b/solution.py
@@ -306,20 +306,29 @@
     sub = lax.broadcasted_iota(jnp.int32, (8, 128), 0)
     lane = lax.broadcasted_iota(jnp.int32, (8, 128), 1)
 
+    def around(h, l, shift_by, ways, axis):
+        turned = [(h, l)] + [
+            (pltpu.roll(h, i * shift_by, axis), pltpu.roll(l, i * shift_by, axis))
+            for i in range(1, ways)
+        ]
+        total, lost = tree_rows([a for a, _ in turned])
+        lows = [b for _, b in turned]
+        while len(lows) > 1:
+            lows = [a + b for a, b in zip(lows[::2], lows[1::2])]
+        return total, lows[0] + lost
+
     def lane_sums(items):
         high = jnp.zeros((8, 128), jnp.float32)
         low = jnp.zeros((8, 128), jnp.float32)
         target = jnp.full((8, 128), 1000, jnp.int32)
         for q, (h, l, place) in enumerate(items):
-            for shift_by in (4, 2, 1):
-                h, e = two_sum(h, pltpu.roll(h, shift_by, 0))
-                l = l + pltpu.roll(l, shift_by, 0) + e
+            for shift_by, ways in ((2, 4), (1, 2)):
+                h, l = around(h, l, shift_by, ways, 0)
             high = jnp.where(sub == q, h, high)
             low = jnp.where(sub == q, l, low)
             target = jnp.where(sub == q, place, target)
-        for shift_by in (64, 32, 16, 8, 4, 2, 1):
-            high, e = two_sum(high, pltpu.roll(high, shift_by, 1))
-            low = low + pltpu.roll(low, shift_by, 1) + e
+        for shift_by, ways in ((32, 4), (8, 4), (2, 4), (1, 2)):
+            high, low = around(high, low, shift_by, ways, 1)
         return jnp.where(lane == target, high, 0.0) + jnp.where(
             lane == target + 16, low, 0.0
         )

time: 78.4 us -> 78.2 us (level)
  no operation moved by 1% of the time
where the time goes in v7:
time: 78.2 us; the launch traced here: 78 us
  Pallas kernels  77.4 us (99%)
    pallas_call x1, Pallas kernels, shards(): pl.pallas_call(functools.partial(iterate, n, group), out_shape=(pltpu.VME...  75.7 us
    pallas_call x1, Pallas kernels, shards(): pl.pallas_call(combine, out_shape=(jax.ShapeDtypeStruct(start_vectors.sha...  1.7 us

profile of v7, /device:TPU:1, one launch (start us, length us, event | category | flops | bytes accessed | tf_op | source)
XLA Modules:
  0.0 78.0 jit_solution(3476793771882425242)
XLA Ops:
  0.6 75.7 %shard_map.66 = (f32[1,128]{1,0:T(1,128)S(1)}, f32[9,2,256,256]{3,2,1,0:T(8,128)S(1)}) custom-call(f32[2,1,256,256]{3,2,1,0:T(8,128)} %sv_ref.1, s32[1,256,256]{2,1,0:T(8,128)} %lev_ref.1, f32[16]{0:T(128)} %en_ref.1), custom_call_target="tpu_custom_call" | custom-call | tf_op jit(solution)/shard_map/pallas_call | solution.py:611
  76.3 1.7 %shard_map.67 = (f32[2,1,256,256]{3,2,1,0:T(8,128)}, f32[2,8]{1,0:T(2,128)}, f32[2,7]{1,0:T(2,128)}, f32[2,6]{1,0:T(2,128)}) custom-call(f32[1,128]{1,0:T(1,128)S(1)} %get-tuple-element.6.row_ref, f32[9,2,256,256]{3,2,1,0:T(8,128)S(1)} %get-tuple-element.7.basis), custom_call_target="tpu_custom_call" | custom-call | tf_op jit(solution)/shard_map/pallas_call | solution.py:645

commit v8 on v7

--- a/solution.py
+++ b/solution.py
@@ -301,7 +301,7 @@
                 added.append((h, l + e))
             return tuple(added)
 
-        return lax.fori_loop(0, count // block_rows, block, totals)
+        return lax.fori_loop(0, count // block_rows, block, totals, unroll=True)
 
     sub = lax.broadcasted_iota(jnp.int32, (8, 128), 0)
     lane = lax.broadcasted_iota(jnp.int32, (8, 128), 1)
@@ -583,7 +583,7 @@
                 field[v, part, :] = value + scale[3] * basis[4, v, part, :]
                 return None
 
-            lax.fori_loop(0, half // BLOCK, finish, None)
+            lax.fori_loop(0, half // BLOCK, finish, None, unroll=True)
             store(v, i).start()
         if v == 0:
             for copy in small:

time: 78.2 us -> 77.5 us (level)
  no operation moved by 1% of the time
where the time goes in v8:
time: 77.5 us; the launch traced here: 77.4 us
  Pallas kernels  76.8 us (99%)
    pallas_call x1, Pallas kernels, shards(): pl.pallas_call(functools.partial(iterate, n, group), out_shape=(pltpu.VME...  75.1 us
    pallas_call x1, Pallas kernels, shards(): pl.pallas_call(combine, out_shape=(jax.ShapeDtypeStruct(start_vectors.sha...  1.62 us

profile of v8, /device:TPU:1, one launch (start us, length us, event | category | flops | bytes accessed | tf_op | source)
XLA Modules:
  0.0 77.4 jit_solution(17716338094736529549)
XLA Ops:
  0.6 75.1 %shard_map.66 = (f32[1,128]{1,0:T(1,128)S(1)}, f32[9,2,256,256]{3,2,1,0:T(8,128)S(1)}) custom-call(f32[2,1,256,256]{3,2,1,0:T(8,128)} %sv_ref.1, s32[1,256,256]{2,1,0:T(8,128)} %lev_ref.1, f32[16]{0:T(128)} %en_ref.1), custom_call_target="tpu_custom_call" | custom-call | tf_op jit(solution)/shard_map/pallas_call | solution.py:611
  75.8 1.6 %shard_map.67 = (f32[2,1,256,256]{3,2,1,0:T(8,128)}, f32[2,8]{1,0:T(2,128)}, f32[2,7]{1,0:T(2,128)}, f32[2,6]{1,0:T(2,128)}) custom-call(f32[1,128]{1,0:T(1,128)S(1)} %get-tuple-element.6.row_ref, f32[9,2,256,256]{3,2,1,0:T(8,128)S(1)} %get-tuple-element.7.basis), custom_call_target="tpu_custom_call" | custom-call | tf_op jit(solution)/shard_map/pallas_call | solution.py:645
